TPU v7x, 32 devices: a whole 2x2x4 slice. The times are simulated.
32 devices in a mesh: gx: 4 (over z), gy: 2 (over y), gz: 4 (over x, core).
Axes of the slice: x: 2, y: 2, z: 4, core: 2. Of those that a mesh axis runs over, the one named last changes fastest.
Arguments:
- positions: float32 [3, 16, 8, 512], P(None, 'gx', 'gy', 'gz'), may hold values from 0.6 to 13.9, as said below
- counts: int32 [16, 8, 8], P('gx', 'gy', 'gz'), may hold values from 24 to 64
Outputs:
- forces: float32 [3, 16, 8, 512], P(None, 'gx', 'gy', 'gz')
- energy: float32 [16, 8, 512], P('gx', 'gy', 'gz')
Inputs may be any that keep to these rules, and one draw needn't show every extreme that they name: `positions`: each cell is a box of 2a x 2a x 4a with a = 3.615 and every atom lies inside its own cell's box; two atoms are 1.0 or more apart, and no atom is within 5.51 of an atom outside its cell's 27 neighbour cells.
All inputs are finite; a program needn't handle non-finite values.
Results may differ from a plain program's by a relative error of at most 0.0003.
Values sent between devices are 32-bit elements; how exact they have to be, the bound alone decides.
A program may use at most 64 MiB of HBM per device.

v0:
```python
import jax
import jax.numpy as jnp
from jax import lax
from jax.sharding import PartitionSpec as P

SLOTS = 64


lattice_const = 3.615
cell_span = (2.0 * lattice_const, 2.0 * lattice_const, 4.0 * lattice_const)
cut_radius = 5.50679
cut_width = 0.50037
dens_scale = 3.80362
beta_one = 0.17394
radius_three = -2.19885
energy_one = 201.458
energy_two = 0.00659288
radius_one = 0.83591
radius_two = 4.46867
alpha_one = 2.97758
alpha_two = 1.54927
shift_delta = 0.0086225
repulsion = ((4.0, 2.24), (40.0, 1.8), (1150.0, 1.2))
embed_zero = -2.28235
embed_curve = 1.35535
lower_terms = (-1.27775, -0.86074, 1.78804, 2.97571)
upper_quartic = 0.4
upper_damping = 0.3
cell_offsets = [
    (first, second, third) for first in (-1, 0, 1) for second in (-1, 0, 1) for third in (-1, 0, 1)
]


def with_halo(value, sides, width):
    for axis, dim in sides:
        count, length = (lax.axis_size(axis), value.shape[dim])
        up = [(i, (i + 1) % count) for i in range(count)]
        down = [(j, i) for i, j in up]
        last = lax.slice_in_dim(value, length - width, length, axis=dim)
        first = lax.slice_in_dim(value, 0, width, axis=dim)
        before = lax.ppermute(last, axis, up)
        after = lax.ppermute(first, axis, down)
        value = jnp.concatenate([before, value, after], axis=dim)
    return value


def tapering(radius):
    scaled = (radius - cut_radius) / cut_width
    quartic = scaled**4
    inside = scaled < 0.0
    taper_value = jnp.where(inside, quartic / (1.0 + quartic), 0.0)
    taper_slope = jnp.where(inside, 4.0 * scaled**3 / (1.0 + quartic) ** 2 / cut_width, 0.0)
    return (taper_value, taper_slope)


def gaussian_part(radius):
    return dens_scale * jnp.exp(-beta_one * (radius - radius_three) ** 2)


def radial_density(radius):
    taper_value, taper_slope = tapering(radius)
    return gaussian_part(radius) * taper_value


def morse_terms(radius, center_at, stiffness):
    decay = jnp.exp(-stiffness * (radius - center_at))
    return (decay * decay - 2.0 * decay, 2.0 * stiffness * (decay - decay * decay))


def pair_terms(radius):
    taper_value, taper_slope = tapering(radius)
    gaussian = gaussian_part(radius)
    dens_value = gaussian * taper_value
    dens_slope = (
        gaussian * (-2.0 * beta_one * (radius - radius_three)) * taper_value
        + gaussian * taper_slope
    )
    morse_first, slope_first = morse_terms(radius, radius_one, alpha_one)
    morse_second, slope_second = morse_terms(radius, radius_two, alpha_two)
    base_value = energy_one * morse_first + energy_two * morse_second + shift_delta
    base_slope = energy_one * slope_first + energy_two * slope_second
    pair_value = base_value * taper_value
    pair_slope = base_slope * taper_value + base_value * taper_slope
    for strength, reach_at in repulsion:
        closeness = jnp.maximum(reach_at - radius, 0.0)
        pair_value = pair_value - strength * closeness**4
        pair_slope = pair_slope + 4.0 * strength * closeness**3
    return (pair_value, pair_slope, dens_value, dens_slope)


def embedding(density):
    excess = density - 1.0
    below_value = (
        embed_zero
        + 0.5 * embed_curve * excess**2
        + lower_terms[0] * excess**3
        + lower_terms[1] * excess**4
        + lower_terms[2] * excess**5
        + lower_terms[3] * excess**6
    )
    below_slope = (
        embed_curve * excess
        + 3.0 * lower_terms[0] * excess**2
        + 4.0 * lower_terms[1] * excess**3
        + 5.0 * lower_terms[2] * excess**4
        + 6.0 * lower_terms[3] * excess**5
    )
    numerator = (
        embed_zero
        + 0.5 * embed_curve * excess**2
        + lower_terms[0] * excess**3
        + upper_quartic * excess**4
    )
    numer_slope = (
        embed_curve * excess + 3.0 * lower_terms[0] * excess**2 + 4.0 * upper_quartic * excess**3
    )
    denominator = 1.0 + upper_damping * excess**3
    above_value = numerator / denominator
    above_slope = (
        numer_slope * denominator - numerator * 3.0 * upper_damping * excess**2
    ) / denominator**2
    is_below = excess < 0.0
    return (
        jnp.where(is_below, below_value, above_value),
        jnp.where(is_below, below_slope, above_slope),
    )


def pair_geometry(center, beside, offset):
    displace = []
    for component in range(3):
        displace.append(
            beside[component][..., None, :]
            + offset[component] * cell_span[component]
            - center[component][..., :, None]
        )
    weight = center[3][..., :, None] * beside[3][..., None, :]
    if offset == (0, 0, 0):
        slot_count = center.shape[-1]
        weight = weight * (1.0 - jnp.eye(slot_count, dtype=jnp.float32))
    squared = displace[0] ** 2 + displace[1] ** 2 + displace[2] ** 2
    radius = jnp.sqrt(jnp.where(weight > 0.0, squared, 100.0))
    return (displace, weight, radius)


def shifted_cells(view_data, offset, extent):
    return view_data[
        :,
        1 + offset[0] : 1 + offset[0] + extent[0],
        1 + offset[1] : 1 + offset[1] + extent[1],
        1 + offset[2] : 1 + offset[2] + extent[2],
    ]


def cell_view(field_data):
    return field_data.reshape(
        field_data.shape[0],
        field_data.shape[1],
        field_data.shape[2],
        field_data.shape[3] // SLOTS,
        SLOTS,
    )


def cell_density(view_data):
    extent = (view_data.shape[1] - 2, view_data.shape[2] - 2, view_data.shape[3] - 2)
    center = view_data[:, 1:-1, 1:-1, 1:-1]
    summed = jnp.zeros(center.shape[1:], jnp.float32)
    for offset in cell_offsets:
        beside = shifted_cells(view_data, offset, extent)
        displace, weight, radius = pair_geometry(center, beside, offset)
        summed = summed + jnp.sum(weight * radial_density(radius), axis=-1)
    return summed


def cell_forces(view_data, slope_data):
    extent = (view_data.shape[1] - 2, view_data.shape[2] - 2, view_data.shape[3] - 2)
    center = view_data[:, 1:-1, 1:-1, 1:-1]
    slope_center = slope_data[0, 1:-1, 1:-1, 1:-1]
    force_sums = [jnp.zeros(center.shape[1:], jnp.float32) for component in range(3)]
    pair_sum = jnp.zeros(center.shape[1:], jnp.float32)
    for offset in cell_offsets:
        beside = shifted_cells(view_data, offset, extent)
        slope_beside = shifted_cells(slope_data, offset, extent)[0]
        displace, weight, radius = pair_geometry(center, beside, offset)
        pair_value, pair_slope, dens_value, dens_slope = pair_terms(radius)
        factor = (
            weight
            * (pair_slope + (slope_center[..., :, None] + slope_beside[..., None, :]) * dens_slope)
            / radius
        )
        force_sums = [
            force_sums[component] + jnp.sum(factor * displace[component], axis=-1)
            for component in range(3)
        ]
        pair_sum = pair_sum + jnp.sum(weight * pair_value, axis=-1)
    return (jnp.stack(force_sums), pair_sum)


def ghosts(field_data):
    along_z = with_halo(field_data, (("gz", 3),), SLOTS)
    return with_halo(along_z, (("gx", 1), ("gy", 2)), 1)


def on_device(positions, counts):
    cells_x, cells_y, cells_z = counts.shape
    occupied = (
        lax.broadcasted_iota(jnp.int32, (cells_x, cells_y, cells_z, SLOTS), 3) < counts[..., None]
    ).astype(jnp.float32)
    packed = jnp.concatenate(
        [positions, occupied.reshape(cells_x, cells_y, cells_z * SLOTS)[None]], axis=0
    )
    view_data = cell_view(ghosts(packed))
    density = cell_density(view_data)
    embed_value, embed_slope = embedding(density)
    slope = embed_slope * occupied
    slope_data = cell_view(ghosts(slope.reshape(1, cells_x, cells_y, cells_z * SLOTS)))
    forces, pair_sum = cell_forces(view_data, slope_data)
    energy = occupied * (embed_value + 0.5 * pair_sum)
    return (
        forces.reshape(3, cells_x, cells_y, cells_z * SLOTS),
        energy.reshape(cells_x, cells_y, cells_z * SLOTS),
    )


def solution(mesh):
    return jax.shard_map(
        on_device,
        mesh=mesh,
        in_specs=(P(None, "gx", "gy", "gz"), P("gx", "gy", "gz")),
        out_specs=(P(None, "gx", "gy", "gz"), P("gx", "gy", "gz")),
        check_vma=False,
    )
```

profile of v0, /device:TPU:0, one launch (start us, length us, event | category | flops | bytes accessed | tf_op | source)
XLA Modules:
  0.0 215.9 jit_solution(4854465897284644223)
XLA Ops:
  0.7 0.8 copy.7
  1.7 0.6 copy-done
  2.4 0.5 collective-permute-start
  2.9 2.0 collective-permute-start.1
  4.9 1.5 collective-permute-done
  6.4 0.2 collective-permute-done.1
  6.7 2.3 %collective-permute-start.2 = (f32[4,1,4,256]{3,2,1,0:T(4,128)S(1)}, f32[4,1,4,256]{3,2,1,0:T(4,128)S(1)}, u32[]{:S(2)}, u32[]{:S(2)}) collective-permute-start(f32[4,1,4,256]{3,2,1,0:T(4,128)S(1)} %get-tuple-element.305), channel_id=1, source_target_pairs={{0,8},{8,16},{16,24},{24,0},{1,9},{9,17},{17,25},{25,1},{2,10},{10... | collective-permute-start | bytes 49160 | tf_op jit(solution)/shard_map/ppermute | solution.py:41
  9.0 2.1 collective-permute-start.3
  11.1 1.8 collective-permute-done.2
  12.9 0.2 pad_maximum_fusion.8
  13.1 1.6 collective-permute-start.4
  14.7 0.5 collective-permute-start.5
  15.2 1.8 collective-permute-done.4
  17.0 1.6 collective-permute-done.5
  18.8 0.2 reshape.1949
  19.8 4.6 %fusion.924 = (f32[4,4,2,64]{3,2,1,0:T(2,128)S(1)}, f32[4,4,2,64]{3,2,1,0:T(2,128)S(1)}, f32[4,4,2,64]{3,2,1,0:T(2,128)S(1)}) fusion(f32[4,4,2,64]{3,2,1,0:T(2,128)S(1)} %get-tuple-element.294, f32[4,4,2,64]{3,2,1,0:T(2,128)S(1)} %get-tuple-element.302, f32[4,4,2,64]{3,2,1,0:T(2,128)S(1)} %get-tuple-element.295, ...), kind=kLoop, calls=%fused_computation.1568 | loop fusion | flops 10217472 | bytes 155648 | tf_op jit(solution)/shard_map/reduce_sum | solution.py:172
  24.6 5.9 %fusion.954 = (f32[4,4,2,64]{3,2,1,0:T(2,128)S(1)}, f32[4,4,2,64]{3,2,1,0:T(2,128)S(1)}, f32[4,4,2,64]{3,2,1,0:T(2,128)S(1)}, f32[4,4,2,64]{3,2,1,0:T(2,128)S(1)}) fusion(f32[4,4,2,64]{3,2,1,0:T(2,128)S(1)} %get-tuple-element.237, f32[4,4,2,64]{3,2,1,0:T(2,128)S(1)} %get-tuple-element.302, f32[4,4,2,64]{3,2,1,0:T(2,128)S(1)} %get-tuple-element.295, ...), kind=kLoop, calls=%fused_computation.1598 | loop fusion | flops 13754368 | bytes 180224 | tf_op jit(solution)/shard_map/reduce_sum | solution.py:172
  30.8 4.6 %fusion.922 = (f32[4,4,2,64]{3,2,1,0:T(2,128)S(1)}, f32[4,4,2,64]{3,2,1,0:T(2,128)S(1)}, f32[4,4,2,64]{3,2,1,0:T(2,128)S(1)}) fusion(f32[4,4,2,64]{3,2,1,0:T(2,128)S(1)} %get-tuple-element.301, f32[4,4,2,64]{3,2,1,0:T(2,128)S(1)} %get-tuple-element.302, f32[4,4,2,64]{3,2,1,0:T(2,128)S(1)} %get-tuple-element.295, ...), kind=kLoop, calls=%fused_computation.1566 | loop fusion | flops 10217472 | bytes 155648 | tf_op jit(solution)/shard_map/reduce_sum | solution.py:172
  35.5 4.6 %fusion.926 = (f32[4,4,2,64]{3,2,1,0:T(2,128)S(1)}, f32[4,4,2,64]{3,2,1,0:T(2,128)S(1)}, f32[4,4,2,64]{3,2,1,0:T(2,128)S(1)}) fusion(f32[4,4,2,64]{3,2,1,0:T(2,128)S(1)} %get-tuple-element.290, f32[4,4,2,64]{3,2,1,0:T(2,128)S(1)} %get-tuple-element.302, f32[4,4,2,64]{3,2,1,0:T(2,128)S(1)} %get-tuple-element.295, ...), kind=kLoop, calls=%fused_computation.1570 | loop fusion | flops 10217472 | bytes 155648 | tf_op jit(solution)/shard_map/reduce_sum | solution.py:172
  40.3 4.6 %fusion.928 = (f32[4,4,2,64]{3,2,1,0:T(2,128)S(1)}, f32[4,4,2,64]{3,2,1,0:T(2,128)S(1)}, f32[4,4,2,64]{3,2,1,0:T(2,128)S(1)}) fusion(f32[4,4,2,64]{3,2,1,0:T(2,128)S(1)} %get-tuple-element.286, f32[4,4,2,64]{3,2,1,0:T(2,128)S(1)} %get-tuple-element.302, f32[4,4,2,64]{3,2,1,0:T(2,128)S(1)} %get-tuple-element.295, ...), kind=kLoop, calls=%fused_computation.1572 | loop fusion | flops 10217472 | bytes 155648 | tf_op jit(solution)/shard_map/reduce_sum | solution.py:172
  45.0 3.3 %fusion.936 = (f32[4,4,2,64]{3,2,1,0:T(2,128)S(1)}, f32[4,4,2,64]{3,2,1,0:T(2,128)S(1)}) fusion(f32[4,4,2,64]{3,2,1,0:T(2,128)S(1)} %get-tuple-element.270, f32[4,4,2,64]{3,2,1,0:T(2,128)S(1)} %get-tuple-element.302, f32[4,4,2,64]{3,2,1,0:T(2,128)S(1)} %get-tuple-element.295, f32[4,4,2,64]{3,2,1,0:T(2,128)S(1)} %get-tuple-element.267, ...), kind=kLoop, calls=%fused_computation.1580 | loop fusion | flops 6811648 | bytes 114688 | tf_op jit(solution)/shard_map/reduce_sum | solution.py:172
  48.4 4.6 %fusion.934 = (f32[4,4,2,64]{3,2,1,0:T(2,128)S(1)}, f32[4,4,2,64]{3,2,1,0:T(2,128)S(1)}, f32[4,4,2,64]{3,2,1,0:T(2,128)S(1)}) fusion(f32[4,4,2,64]{3,2,1,0:T(2,128)S(1)} %get-tuple-element.274, f32[4,4,2,64]{3,2,1,0:T(2,128)S(1)} %get-tuple-element.302, f32[4,4,2,64]{3,2,1,0:T(2,128)S(1)} %get-tuple-element.295, ...), kind=kLoop, calls=%fused_computation.1578 | loop fusion | flops 10217472 | bytes 155648 | tf_op jit(solution)/shard_map/reduce_sum | solution.py:172
  53.0 4.6 %fusion.932 = (f32[4,4,2,64]{3,2,1,0:T(2,128)S(1)}, f32[4,4,2,64]{3,2,1,0:T(2,128)S(1)}, f32[4,4,2,64]{3,2,1,0:T(2,128)S(1)}) fusion(f32[4,4,2,64]{3,2,1,0:T(2,128)S(1)} %get-tuple-element.278, f32[4,4,2,64]{3,2,1,0:T(2,128)S(1)} %get-tuple-element.302, f32[4,4,2,64]{3,2,1,0:T(2,128)S(1)} %get-tuple-element.295, ...), kind=kLoop, calls=%fused_computation.1576 | loop fusion | flops 10217472 | bytes 155648 | tf_op jit(solution)/shard_map/reduce_sum | solution.py:172
  57.6 4.6 %fusion.930 = (f32[4,4,2,64]{3,2,1,0:T(2,128)S(1)}, f32[4,4,2,64]{3,2,1,0:T(2,128)S(1)}, f32[4,4,2,64]{3,2,1,0:T(2,128)S(1)}) fusion(f32[4,4,2,64]{3,2,1,0:T(2,128)S(1)} %get-tuple-element.282, f32[4,4,2,64]{3,2,1,0:T(2,128)S(1)} %get-tuple-element.302, f32[4,4,2,64]{3,2,1,0:T(2,128)S(1)} %get-tuple-element.295, ...), kind=kLoop, calls=%fused_computation.1574 | loop fusion | flops 10217472 | bytes 155648 | tf_op jit(solution)/shard_map/reduce_sum | solution.py:172
  62.5 1.7 collective-permute-start.7
  64.3 1.3 collective-permute-done.6
  65.7 1.4 collective-permute-start.8
  67.1 2.4 %collective-permute-start.9 = (f32[1,1,4,256]{3,2,1,0:T(4,128)S(1)}, f32[1,1,4,256]{3,2,1,0:T(4,128)S(1)}, u32[]{:S(2)}, u32[]{:S(2)}) collective-permute-start(f32[1,1,4,256]{3,2,1,0:T(4,128)S(1)} %get-tuple-element.339), channel_id=1, source_target_pairs={{8,0},{16,8},{24,16},{0,24},{9,1},{17,9},{25,17},{1,25},{10,2},{18... | collective-permute-start | bytes 12296 | tf_op jit(solution)/shard_map/ppermute | solution.py:42
  69.6 1.5 collective-permute-done.8
  71.2 0.5 collective-permute-start.10
  71.7 1.6 collective-permute-start.11
  74.3 0.6 collective-permute-done.10
  74.9 0.5 collective-permute-done.11
  75.7 10.2 %fusion.314 = (f32[4,4,2,64]{3,2,1,0:T(2,128)S(1)}, f32[4,4,2,64]{3,2,1,0:T(2,128)S(1)}, f32[4,4,2,64]{3,2,1,0:T(2,128)S(1)}, f32[4,4,2,64]{3,2,1,0:T(2,128)S(1)...) fusion(f32[4,4,2,64]{3,2,1,0:T(2,128)S(1)} %get-tuple-element.2, ...), kind=kLoop, calls=%fused_computation.958 | loop fusion | flops 25411584 | bytes 188416 | tf_op jit(solution)/shard_map/reduce_sum | solution.py:193
  86.0 10.0 %fusion.290 = (f32[4,4,2,64]{3,2,1,0:T(2,128)S(1)}, f32[4,4,2,64]{3,2,1,0:T(2,128)S(1)}, f32[4,4,2,64]{3,2,1,0:T(2,128)S(1)}, f32[4,4,2,64]{3,2,1,0:T(2,128)S(1)...) fusion(f32[4,4,2,64]{3,2,1,0:T(2,128)S(1)} %get-tuple-element.2, ...), kind=kLoop, calls=%fused_computation.934 | loop fusion | flops 25411584 | bytes 188416 | tf_op jit(solution)/shard_map/reduce_sum | solution.py:193
  96.1 10.0 %fusion.266 = (f32[4,4,2,64]{3,2,1,0:T(2,128)S(1)}, f32[4,4,2,64]{3,2,1,0:T(2,128)S(1)}, f32[4,4,2,64]{3,2,1,0:T(2,128)S(1)}, f32[4,4,2,64]{3,2,1,0:T(2,128)S(1)...) fusion(f32[4,4,2,64]{3,2,1,0:T(2,128)S(1)} %get-tuple-element.2, ...), kind=kLoop, calls=%fused_computation.910 | loop fusion | flops 25411584 | bytes 188416 | tf_op jit(solution)/shard_map/reduce_sum | solution.py:193
  106.3 10.0 %fusion.242 = (f32[4,4,2,64]{3,2,1,0:T(2,128)S(1)}, f32[4,4,2,64]{3,2,1,0:T(2,128)S(1)}, f32[4,4,2,64]{3,2,1,0:T(2,128)S(1)}, f32[4,4,2,64]{3,2,1,0:T(2,128)S(1)...) fusion(f32[4,4,2,64]{3,2,1,0:T(2,128)S(1)} %get-tuple-element.2, ...), kind=kLoop, calls=%fused_computation.886 | loop fusion | flops 25411584 | bytes 188416 | tf_op jit(solution)/shard_map/reduce_sum | solution.py:193
  116.4 10.0 %fusion.110 = (f32[4,4,2,64]{3,2,1,0:T(2,128)S(1)}, f32[4,4,2,64]{3,2,1,0:T(2,128)S(1)}, f32[4,4,2,64]{3,2,1,0:T(2,128)S(1)}, f32[4,4,2,64]{3,2,1,0:T(2,128)S(1)...) fusion(f32[4,4,2,64]{3,2,1,0:T(2,128)S(1)} %get-tuple-element.2, ...), kind=kLoop, calls=%fused_computation.754 | loop fusion | flops 25411584 | bytes 188416 | tf_op jit(solution)/shard_map/reduce_sum | solution.py:193
  126.4 10.0 %fusion.86 = (f32[4,4,2,64]{3,2,1,0:T(2,128)S(1)}, f32[4,4,2,64]{3,2,1,0:T(2,128)S(1)}, f32[4,4,2,64]{3,2,1,0:T(2,128)S(1)}, f32[4,4,2,64]{3,2,1,0:T(2,128)S(1)}...) fusion(f32[4,4,2,64]{3,2,1,0:T(2,128)S(1)} %get-tuple-element.2, ...), kind=kLoop, calls=%fused_computation.730 | loop fusion | flops 25411584 | bytes 188416 | tf_op jit(solution)/shard_map/reduce_sum | solution.py:193
  136.5 10.0 %fusion.62 = (f32[4,4,2,64]{3,2,1,0:T(2,128)S(1)}, f32[4,4,2,64]{3,2,1,0:T(2,128)S(1)}, f32[4,4,2,64]{3,2,1,0:T(2,128)S(1)}, f32[4,4,2,64]{3,2,1,0:T(2,128)S(1)}...) fusion(f32[4,4,2,64]{3,2,1,0:T(2,128)S(1)} %get-tuple-element.2, ...), kind=kLoop, calls=%fused_computation.706 | loop fusion | flops 25411584 | bytes 188416 | tf_op jit(solution)/shard_map/reduce_sum | solution.py:193
  146.5 10.0 %fusion.4 = (f32[4,4,2,64]{3,2,1,0:T(2,128)S(1)}, f32[4,4,2,64]{3,2,1,0:T(2,128)S(1)}, f32[4,4,2,64]{3,2,1,0:T(2,128)S(1)}, f32[4,4,2,64]{3,2,1,0:T(2,128)S(1)},...) fusion(f32[4,4,2,64]{3,2,1,0:T(2,128)S(1)} %get-tuple-element.2, ...), kind=kLoop, calls=%fused_computation.648 | loop fusion | flops 25411584 | bytes 188416 | tf_op jit(solution)/shard_map/reduce_sum | solution.py:193
  156.6 10.3 %fusion.218 = (f32[4,4,2,64]{3,2,1,0:T(2,128)S(1)}, f32[4,4,2,64]{3,2,1,0:T(2,128)S(1)}, f32[4,4,2,64]{3,2,1,0:T(2,128)S(1)}, f32[4,4,2,64]{3,2,1,0:T(2,128)S(1)...) fusion(f32[4,4,2,64]{3,2,1,0:T(2,128)S(1)} %get-tuple-element.2, ...), kind=kLoop, calls=%fused_computation.862 | loop fusion | flops 25411584 | bytes 188416 | tf_op jit(solution)/shard_map/reduce_sum | solution.py:193
  166.9 10.0 %fusion.194 = (f32[4,4,2,64]{3,2,1,0:T(2,128)S(1)}, f32[4,4,2,64]{3,2,1,0:T(2,128)S(1)}, f32[4,4,2,64]{3,2,1,0:T(2,128)S(1)}, f32[4,4,2,64]{3,2,1,0:T(2,128)S(1)...) fusion(f32[4,4,2,64]{3,2,1,0:T(2,128)S(1)} %get-tuple-element.2, ...), kind=kLoop, calls=%fused_computation.838 | loop fusion | flops 25411584 | bytes 188416 | tf_op jit(solution)/shard_map/reduce_sum | solution.py:193
  176.9 10.0 %fusion.158 = (f32[4,4,2,64]{3,2,1,0:T(2,128)S(1)}, f32[4,4,2,64]{3,2,1,0:T(2,128)S(1)}, f32[4,4,2,64]{3,2,1,0:T(2,128)S(1)}, f32[4,4,2,64]{3,2,1,0:T(2,128)S(1)...) fusion(f32[4,4,2,64]{3,2,1,0:T(2,128)S(1)} %get-tuple-element.2, ...), kind=kLoop, calls=%fused_computation.802 | loop fusion | flops 25411584 | bytes 188416 | tf_op jit(solution)/shard_map/reduce_sum | solution.py:193
  187.0 10.0 %fusion.134 = (f32[4,4,2,64]{3,2,1,0:T(2,128)S(1)}, f32[4,4,2,64]{3,2,1,0:T(2,128)S(1)}, f32[4,4,2,64]{3,2,1,0:T(2,128)S(1)}, f32[4,4,2,64]{3,2,1,0:T(2,128)S(1)...) fusion(f32[4,4,2,64]{3,2,1,0:T(2,128)S(1)} %get-tuple-element.2, ...), kind=kLoop, calls=%fused_computation.778 | loop fusion | flops 25411584 | bytes 188416 | tf_op jit(solution)/shard_map/reduce_sum | solution.py:193
  197.0 13.9 %fusion.182 = (f32[4,4,2,64]{3,2,1,0:T(2,128)S(1)}, f32[4,4,2,64]{3,2,1,0:T(2,128)S(1)}, f32[4,4,2,64]{3,2,1,0:T(2,128)S(1)}, f32[4,4,2,64]{3,2,1,0:T(2,128)S(1)...) fusion(f32[4,4,2,64]{3,2,1,0:T(2,128)S(1)} %get-tuple-element.2, ...), kind=kLoop, calls=%fused_computation.826 | loop fusion | flops 38248448 | bytes 237568 | tf_op jit(solution)/shard_map/reduce_sum | solution.py:193
  214.6 0.6 pad_maximum_fusion.9
  215.2 0.6 fusion.1104
  (104 shorter events, 8.1 us)
Async XLA Ops:
  1.6 0.7 copy-start
  2.4 4.0 %collective-permute-start = (f32[4,4,4,64]{3,2,1,0:T(4,128)S(1)}, f32[4,4,4,64]{3,2,1,0:T(4,128)S(1)}, u32[]{:S(2)}, u32[]{:S(2)}) collective-permute-start(f32[4,4,4,64]{3,2,1,0:T(4,128)S(1)} %get-tuple-element.336), channel_id=1, source_target_pairs={{0,1},{1,2},{2,3},{3,0},{4,5},{5,6},{6,7},{7,4},{8,9},{9,10},{10,1... | collective-permute-start | bytes 49160 | tf_op jit(solution)/shard_map/ppermute | solution.py:41
  2.9 3.7 %collective-permute-start.1 = (f32[4,4,4,64]{3,2,1,0:T(4,128)S(1)}, f32[4,4,4,64]{3,2,1,0:T(4,128)S(1)}, u32[]{:S(2)}, u32[]{:S(2)}) collective-permute-start(f32[4,4,4,64]{3,2,1,0:T(4,128)S(1)} %get-tuple-element.337), channel_id=1, source_target_pairs={{1,0},{2,1},{3,2},{0,3},{5,4},{6,5},{7,6},{4,7},{9,8},{10,9},{11,1... | collective-permute-start | bytes 49160 | tf_op jit(solution)/shard_map/ppermute | solution.py:42
  6.7 6.1 %collective-permute-start.2 = (f32[4,1,4,256]{3,2,1,0:T(4,128)S(1)}, f32[4,1,4,256]{3,2,1,0:T(4,128)S(1)}, u32[]{:S(2)}, u32[]{:S(2)}) collective-permute-start(f32[4,1,4,256]{3,2,1,0:T(4,128)S(1)} %get-tuple-element.305), channel_id=1, source_target_pairs={{0,8},{8,16},{16,24},{24,0},{1,9},{9,17},{17,25},{25,1},{2,10},{10... | collective-permute-start | bytes 49160 | tf_op jit(solution)/shard_map/ppermute | solution.py:41
  9.0 3.9 %collective-permute-start.3 = (f32[4,1,4,256]{3,2,1,0:T(4,128)S(1)}, f32[4,1,4,256]{3,2,1,0:T(4,128)S(1)}, u32[]{:S(2)}, u32[]{:S(2)}) collective-permute-start(f32[4,1,4,256]{3,2,1,0:T(4,128)S(1)} %get-tuple-element.306), channel_id=1, source_target_pairs={{8,0},{16,8},{24,16},{0,24},{9,1},{17,9},{25,17},{1,25},{10,2},{18... | collective-permute-start | bytes 49160 | tf_op jit(solution)/shard_map/ppermute | solution.py:42
  13.1 3.9 %collective-permute-start.4 = (f32[4,6,1,256]{3,2,1,0:T(1,128)S(1)}, f32[4,6,1,256]{3,2,1,0:T(1,128)S(1)}, u32[]{:S(2)}, u32[]{:S(2)}) collective-permute-start(f32[4,6,1,256]{3,2,1,0:T(1,128)S(1)} %get-tuple-element.303), channel_id=1, source_target_pairs={{0,4},{4,0},{1,5},{5,1},{2,6},{6,2},{3,7},{7,3},{8,12},{12,8},{9,1... | collective-permute-start | bytes 73736 | tf_op jit(solution)/shard_map/ppermute | solution.py:41
  14.7 3.8 %collective-permute-start.5 = (f32[4,6,1,256]{3,2,1,0:T(1,128)S(1)}, f32[4,6,1,256]{3,2,1,0:T(1,128)S(1)}, u32[]{:S(2)}, u32[]{:S(2)}) collective-permute-start(f32[4,6,1,256]{3,2,1,0:T(1,128)S(1)} %get-tuple-element.304), channel_id=1, source_target_pairs={{4,0},{0,4},{5,1},{1,5},{6,2},{2,6},{7,3},{3,7},{12,8},{8,12},{13,... | collective-permute-start | bytes 73736 | tf_op jit(solution)/shard_map/ppermute | solution.py:42
  62.5 3.1 %collective-permute-start.6 = (f32[1,4,4,64]{3,2,1,0:T(4,128)S(1)}, f32[1,4,4,64]{3,2,1,0:T(4,128)S(1)}, u32[]{:S(2)}, u32[]{:S(2)}) collective-permute-start(f32[1,4,4,64]{3,2,1,0:T(4,128)S(1)} %get-tuple-element.340), channel_id=1, source_target_pairs={{0,1},{1,2},{2,3},{3,0},{4,5},{5,6},{6,7},{7,4},{8,9},{9,10},{10,1... | collective-permute-start | bytes 12296 | tf_op jit(solution)/shard_map/ppermute | solution.py:41
  62.5 3.1 %collective-permute-start.7 = (f32[1,4,4,64]{3,2,1,0:T(4,128)S(1)}, f32[1,4,4,64]{3,2,1,0:T(4,128)S(1)}, u32[]{:S(2)}, u32[]{:S(2)}) collective-permute-start(f32[1,4,4,64]{3,2,1,0:T(4,128)S(1)} %get-tuple-element.341), channel_id=1, source_target_pairs={{1,0},{2,1},{3,2},{0,3},{5,4},{6,5},{7,6},{4,7},{9,8},{10,9},{11,1... | collective-permute-start | bytes 12296 | tf_op jit(solution)/shard_map/ppermute | solution.py:42
  65.7 5.4 %collective-permute-start.8 = (f32[1,1,4,256]{3,2,1,0:T(4,128)S(1)}, f32[1,1,4,256]{3,2,1,0:T(4,128)S(1)}, u32[]{:S(2)}, u32[]{:S(2)}) collective-permute-start(f32[1,1,4,256]{3,2,1,0:T(4,128)S(1)} %get-tuple-element.338), channel_id=1, source_target_pairs={{0,8},{8,16},{16,24},{24,0},{1,9},{9,17},{17,25},{25,1},{2,10},{10... | collective-permute-start | bytes 12296 | tf_op jit(solution)/shard_map/ppermute | solution.py:41
  67.1 4.0 %collective-permute-start.9 = (f32[1,1,4,256]{3,2,1,0:T(4,128)S(1)}, f32[1,1,4,256]{3,2,1,0:T(4,128)S(1)}, u32[]{:S(2)}, u32[]{:S(2)}) collective-permute-start(f32[1,1,4,256]{3,2,1,0:T(4,128)S(1)} %get-tuple-element.339), channel_id=1, source_target_pairs={{8,0},{16,8},{24,16},{0,24},{9,1},{17,9},{25,17},{1,25},{10,2},{18... | collective-permute-start | bytes 12296 | tf_op jit(solution)/shard_map/ppermute | solution.py:42
  71.2 3.7 %collective-permute-start.10 = (f32[1,6,1,256]{3,2,1,0:T(1,128)S(1)}, f32[1,6,1,256]{3,2,1,0:T(1,128)S(1)}, u32[]{:S(2)}, u32[]{:S(2)}) collective-permute-start(f32[1,6,1,256]{3,2,1,0:T(1,128)S(1)} %get-tuple-element.334), channel_id=1, source_target_pairs={{0,4},{4,0},{1,5},{5,1},{2,6},{6,2},{3,7},{7,3},{8,12},{12,8},{9,1... | collective-permute-start | bytes 18440 | tf_op jit(solution)/shard_map/ppermute | solution.py:41
  71.7 3.6 %collective-permute-start.11 = (f32[1,6,1,256]{3,2,1,0:T(1,128)S(1)}, f32[1,6,1,256]{3,2,1,0:T(1,128)S(1)}, u32[]{:S(2)}, u32[]{:S(2)}) collective-permute-start(f32[1,6,1,256]{3,2,1,0:T(1,128)S(1)} %get-tuple-element.335), channel_id=1, source_target_pairs={{4,0},{0,4},{5,1},{1,5},{6,2},{2,6},{7,3},{3,7},{12,8},{8,12},{13,... | collective-permute-start | bytes 18440 | tf_op jit(solution)/shard_map/ppermute | solution.py:42
where the time goes:
time: 216 us
  other arithmetic  179 us (83%)
  starting transfers between devices  16.7 us (8%)
  waiting for transfers between devices  10.8 us (5%)
  local copies, waits for them, and re-layouts  8.04 us (4%)
    reduce_sum x13, other arithmetic, cell_forces(): jnp.sum(factor * displace[component], axis=-1)  135 us
    reduce_sum x9, other arithmetic, cell_density(): summed = summed + jnp.sum(weight * radial_density(radius), axis=-1)  41.5 us
    ppermute x6, starting transfers between devices, with_halo(): after = lax.ppermute(first, axis, down)  10.3 us
    ppermute x6, waiting for transfers between devices, with_halo(): before = lax.ppermute(last, axis, up)  8.5 us
    ppermute x6, starting transfers between devices, with_halo(): before = lax.ppermute(last, axis, up)  6.38 us
  transfers between devices with their start and end apart: 12, of which 10 were waited for; matrix products, arithmetic and copies ran while one was open for 0% of the time, Pallas kernels for 0%

commit v1 on v0

v1 whole, which is shorter than its diff:
```python
import functools
import math

import jax
import jax.numpy as jnp
from jax import lax
from jax.experimental import pallas as pl
from jax.experimental.pallas import tpu as pltpu
from jax.sharding import PartitionSpec as P

SLOTS = 64
LANES = 128
FAR = 1.0e4

lattice_const = 3.615
cell_span = (2.0 * lattice_const, 2.0 * lattice_const, 4.0 * lattice_const)
cut_radius = 5.50679
cut_width = 0.50037
dens_scale = 3.80362
beta_one = 0.17394
radius_three = -2.19885
energy_one = 201.458
energy_two = 0.00659288
radius_one = 0.83591
radius_two = 4.46867
alpha_one = 2.97758
alpha_two = 1.54927
shift_delta = 0.0086225
repulsion = ((4.0, 2.24), (40.0, 1.8), (1150.0, 1.2))
embed_zero = -2.28235
embed_curve = 1.35535
lower_terms = (-1.27775, -0.86074, 1.78804, 2.97571)
upper_quartic = 0.4
upper_damping = 0.3
LOG2E = math.log2(math.e)
KEEP_SQUARED = 5.5075**2
ROWS = 16
WIDE = 2


def embedding(density):
    excess = density - 1.0
    square = excess * excess
    cube = square * excess
    below_value = embed_zero + square * (
        0.5 * embed_curve
        + excess
        * (lower_terms[0] + excess * (lower_terms[1] + excess * (lower_terms[2] + excess * lower_terms[3])))
    )
    below_slope = excess * (
        embed_curve
        + excess
        * (
            3.0 * lower_terms[0]
            + excess * (4.0 * lower_terms[1] + excess * (5.0 * lower_terms[2] + excess * 6.0 * lower_terms[3]))
        )
    )
    numerator = embed_zero + square * (0.5 * embed_curve + excess * (lower_terms[0] + excess * upper_quartic))
    numer_slope = excess * (embed_curve + excess * (3.0 * lower_terms[0] + excess * 4.0 * upper_quartic))
    is_below = excess < 0.0
    denominator = jnp.where(is_below, 1.0, 1.0 + upper_damping * cube)
    above_value = numerator / denominator
    above_slope = (numer_slope - above_value * (3.0 * upper_damping) * square) / denominator
    return (
        jnp.where(is_below, below_value, above_value),
        jnp.where(is_below, below_slope, above_slope),
    )


def iota(shape, dim):
    return lax.broadcasted_iota(jnp.int32, shape, dim)


def compress_cell(halo_ref, cx, cy, cz, ny):
    shape = (8, LANES)
    row = iota(shape, 0)
    lane = iota(shape, 1)
    comp = row // 2
    odd = row % 2
    layer = jnp.where(odd == 0, jnp.where(lane < SLOTS, 0, 1), jnp.where(lane < SLOTS, 2, -1))
    is_x, is_y, is_z = (comp == 0, comp == 1, comp == 2)
    add_z = jnp.where(is_z, (layer - cz).astype(jnp.float32) * cell_span[2], 0.0)
    span = jnp.where(is_z, cell_span[2], jnp.where(is_y, cell_span[1], cell_span[0]))
    counted = comp < 3
    data, drops = ([], [])
    for o1 in (-1, 0, 1):
        for o2 in (-1, 0, 1):
            add = jnp.where(is_x, o1 * cell_span[0], jnp.where(is_y, o2 * cell_span[1], add_z))
            value = halo_ref[(cx + 1 + o1) * ny + cy + 1 + o2] + add
            gap = jnp.maximum(jnp.maximum(-value, value - span), 0.0)
            gap = jnp.where(counted, gap * gap, 0.0)
            gap = gap + pltpu.roll(gap, 4, 0)
            gap = gap + pltpu.roll(gap, 2, 0)
            data.append(value)
            drops.append(gap >= KEEP_SQUARED)
    dropped = jnp.concatenate([jnp.where(d, 1.0, 0.0) for d in drops], axis=0).astype(jnp.bfloat16)
    pre = jnp.where(iota((LANES, 2 * LANES), 1) >= LANES, 1.0, 0.0)
    pre = jnp.where(iota((LANES, 2 * LANES), 0) < iota((LANES, 2 * LANES), 1), 1.0, pre)
    sums = jnp.dot(dropped, pre.astype(jnp.bfloat16), preferred_element_type=jnp.float32)
    sums = sums.astype(jnp.int32)
    outs = []
    counts = jnp.zeros((1, LANES), jnp.int32)
    one_row = iota((1, LANES), 1)
    for k in range(9):
        value = data[k]
        move = jnp.where(drops[k], 0, sums[8 * k : 8 * k + 8, :LANES])
        for bit in range(7):
            step = 1 << bit
            value_in = pltpu.roll(value, LANES - step, 1)
            move_in = pltpu.roll(move, LANES - step, 1)
            comes = (move_in & step) != 0
            value = jnp.where(comes, value_in, value)
            move = jnp.where(comes, move_in, jnp.where((move & step) != 0, 0, move))
        outs.append(value)
        total = LANES - sums[8 * k : 8 * k + 8, LANES:]
        counts = jnp.where(one_row == 2 * k, total[0:1], counts)
        counts = jnp.where(one_row == 2 * k + 1, total[1:2], counts)
    return outs, counts


def merge_cell(packed_ref, count_ref, list_ref, cell):
    lane = iota((8, LANES), 1)
    offset = jnp.int32(0)
    current = jnp.zeros((8, LANES), jnp.float32)
    for k in range(18):
        number = count_ref[cell, k]
        tile = offset // LANES
        place = offset % LANES
        turned = pltpu.roll(packed_ref[cell * 18 + k], place, 1)
        current = jnp.where(lane >= place, turned, current)
        list_ref[tile] = current
        current = jnp.where(lane < place + number - LANES, turned, current)
        offset = offset + number
    tile = offset // LANES
    place = offset % LANES
    list_ref[tile] = jnp.where(lane >= place, FAR, current)
    for extra in range(1, WIDE):
        list_ref[tile + extra] = jnp.full((8, LANES), FAR, jnp.float32)
    return (offset + WIDE * LANES - 1) // (WIDE * LANES)


def taper_parts(radius):
    scaled = jnp.minimum(radius * (1.0 / cut_width) - cut_radius / cut_width, 0.0)
    square = scaled * scaled
    quartic = square * square
    inverse = pl.reciprocal(1.0 + quartic, approx=False)
    return scaled, square, quartic * inverse, inverse


def gaussian(radius):
    scale = math.sqrt(beta_one * LOG2E)
    along = radius * scale - radius_three * scale
    return along, jnp.exp2(math.log2(dens_scale) - along * along)


def pair_body(kind, centers, slope_i, tile):
    d = [tile[2 * c : 2 * c + 1] - centers[c] for c in range(3)]
    squared = d[0] * d[0] + d[1] * d[1] + d[2] * d[2]
    squared = jnp.where(squared < 0.25, 100.0, squared)
    inv = lax.rsqrt(squared)
    radius = squared * inv
    scaled, square, taper, inverse = taper_parts(radius)
    along, gauss = gaussian(radius)
    if kind == 0:
        return [gauss * taper]
    taper_slope = (square * scaled) * (inverse * inverse) * (4.0 / cut_width)
    scale = math.sqrt(beta_one * LOG2E)
    dens_slope = gauss * (taper_slope - (along * (2.0 * beta_one / scale)) * taper)
    u = jnp.exp2(radius * (-alpha_one * LOG2E) + alpha_one * LOG2E * radius_one)
    v = jnp.exp2(radius * (-alpha_two * LOG2E) + alpha_two * LOG2E * radius_two)
    a = u * u - u
    b = v * v - v
    base = energy_one * (a - u) + (energy_two * (b - v) + shift_delta)
    base_slope = (-2.0 * alpha_one * energy_one) * a + (-2.0 * alpha_two * energy_two) * b
    pair_value = base * taper
    pair_slope = base_slope * taper + base * taper_slope
    quarter = None
    for strength, reach in repulsion:
        close = jnp.maximum(reach - radius, 0.0)
        cubed = (4.0 * strength) * (close * close * close)
        pair_slope = pair_slope + cubed
        quarter = cubed * close if quarter is None else quarter + cubed * close
    pair_value = pair_value - 0.25 * quarter
    factor = (pair_slope + (slope_i + tile[6:7]) * dens_slope) * inv
    return [pair_value, factor * d[0], factor * d[1], factor * d[2]]


def fold(value):
    total = value[:, :LANES]
    for k in range(1, WIDE):
        total = total + value[:, k * LANES : (k + 1) * LANES]
    return total


def pair_kernel(kind, dims, *refs):
    if kind == 0:
        own_ref, halo_ref, embed_ref, slope_ref = refs[:4]
        rest = refs[4:]
    else:
        own_ref, halo_ref, embed_ref, force_ref, energy_ref = refs[:5]
        rest = refs[5:]
    packed_ref, count_vmem, count_ref, list_ref, column_ref, sum_ref, sem = rest
    cells_x, cells_y = dims
    columns = cells_x * cells_y
    cells = 2 * columns
    ny = cells_y + 2
    number = 1 if kind == 0 else 4

    @pl.loop(0, cells)
    def _(cell):
        column = cell // 2
        outs, counts = compress_cell(halo_ref, column // cells_y, column % cells_y, cell % 2, ny)
        for k in range(9):
            packed_ref[cell * 18 + 2 * k] = outs[k]
            packed_ref[cell * 18 + 2 * k + 1] = pltpu.roll(outs[k], 7, 0)
        count_vmem[pl.ds(cell, 1), :] = counts

    copy = pltpu.make_async_copy(count_vmem, count_ref, sem)
    copy.start()

    @pl.loop(0, columns)
    def _(column):
        value = halo_ref[(column // cells_y + 1) * ny + column % cells_y + 1]
        column_ref[column] = jnp.transpose(jnp.concatenate([value] * 16, axis=0))

    copy.wait()

    @pl.loop(0, cells)
    def _(cell):
        column = cell // 2
        begin = (cell % 2) * SLOTS
        steps = merge_cell(packed_ref, count_ref, list_ref, cell)
        blocks = (own_ref[cell] + ROWS - 1) // ROWS

        @pl.loop(0, blocks)
        def _(block):
            start = pl.multiple_of(begin + block * ROWS, ROWS)
            held = column_ref[column, pl.ds(start, ROWS), :]
            wide = (ROWS, WIDE * LANES)
            centers = [jnp.broadcast_to(held[:, 2 * c : 2 * c + 1], wide) for c in range(3)]
            slope_i = jnp.broadcast_to(held[:, 6:7], wide) if kind else None

            def step(index, sums):
                tile = jnp.concatenate([list_ref[index * WIDE + k] for k in range(WIDE)], axis=1)
                parts = pair_body(kind, centers, slope_i, tile)
                return tuple(s + fold(p) for s, p in zip(sums, parts))

            zero = jnp.zeros((ROWS, LANES), jnp.float32)
            sums = lax.fori_loop(0, steps, step, (zero,) * number)
            for k in range(number):
                sum_ref[k, column, pl.ds(start, ROWS), :] = sums[k]

    ones = jnp.ones((8, LANES), jnp.float32)
    totals = []
    for column in range(columns):
        value = halo_ref[(column // cells_y + 1) * ny + column % cells_y + 1]
        filled = value[0:1] < 0.5 * FAR
        rows = []
        for k in range(number):
            total = lax.dot_general(
                ones,
                sum_ref[k, column],
                (((1,), (1,)), ((), ())),
                precision=lax.Precision.HIGHEST,
                preferred_element_type=jnp.float32,
            )
            rows.append(jnp.where(filled, total[0:1], 0.0))
        totals.append((rows, filled))
    if kind == 0:
        density = jnp.concatenate([t[0][0] for t in totals], axis=0)
        filled = jnp.concatenate([jnp.where(t[1], 1.0, 0.0) for t in totals], axis=0)
        embed_value, embed_slope = embedding(density)
        embed_ref[...] = embed_value
        slope_ref[...] = embed_slope * filled
    else:
        filled = jnp.concatenate([jnp.where(t[1], 1.0, 0.0) for t in totals], axis=0)
        pair_sum = jnp.concatenate([t[0][0] for t in totals], axis=0)
        energy_ref[...] = filled * (embed_ref[...] + 0.5 * pair_sum)
        for c in range(3):
            force_ref[c] = jnp.concatenate([t[0][1 + c] for t in totals], axis=0)


def call_pairs(kind, dims, own, halo, embed=None):
    cells_x, cells_y = dims
    columns = cells_x * cells_y
    cells = 2 * columns
    flat = jax.ShapeDtypeStruct((columns, LANES), jnp.float32)
    vmem = pl.BlockSpec(memory_space=pltpu.VMEM)
    smem = pl.BlockSpec(memory_space=pltpu.SMEM)
    if kind == 0:
        outs, args = ((flat, flat), (own, halo))
    else:
        outs = (jax.ShapeDtypeStruct((3, columns, LANES), jnp.float32), flat)
        args = (own, halo, embed)
    number = 1 if kind == 0 else 4
    return pl.pallas_call(
        functools.partial(pair_kernel, kind, dims),
        out_shape=outs,
        in_specs=[smem] + [vmem] * (len(args) - 1),
        out_specs=(vmem, vmem),
        scratch_shapes=[
            pltpu.VMEM((cells * 18, 8, LANES), jnp.float32),
            pltpu.VMEM((cells, LANES), jnp.int32),
            pltpu.SMEM((cells, LANES), jnp.int32),
            pltpu.VMEM((18 + WIDE + 1, 8, LANES), jnp.float32),
            pltpu.VMEM((columns, LANES, LANES), jnp.float32),
            pltpu.VMEM((number, columns, LANES, LANES), jnp.float32),
            pltpu.SemaphoreType.DMA,
        ],
        compiler_params=pltpu.CompilerParams(vmem_limit_bytes=48 * 1024 * 1024),
        name="density" if kind == 0 else "forces",
    )(*args)


def swap(value, axis, dim, low, high):
    count = lax.axis_size(axis)
    up = [(i, (i + 1) % count) for i in range(count)]
    down = [(j, i) for i, j in up]
    before = lax.ppermute(high, axis, up)
    after = lax.ppermute(low, axis, down)
    return before, after


def ghosts(value):
    before, after = swap(value, "gz", 3, value[..., :SLOTS], value[..., SLOTS:])
    value = jnp.stack([value, jnp.concatenate([after, before], axis=-1)], axis=3)
    before, after = swap(value, "gx", 0, value[:1], value[-1:])
    value = jnp.concatenate([before, value, after], axis=0)
    before, after = swap(value, "gy", 1, value[:, :1], value[:, -1:])
    value = jnp.concatenate([before, value, after], axis=1)
    nx, ny, comps = value.shape[:3]
    return value.reshape(nx * ny, 2 * comps, LANES)


def on_device(positions, counts):
    cells_x, cells_y, cells_z = counts.shape
    dims = (cells_x, cells_y)
    occupied = lax.broadcasted_iota(jnp.int32, (cells_x, cells_y, cells_z, SLOTS), 3) < counts[..., None]
    occupied = occupied.reshape(1, cells_x, cells_y, cells_z * SLOTS)
    placed = jnp.where(occupied, positions, FAR)
    around = ghosts(jnp.transpose(placed, (1, 2, 0, 3)))
    own = counts.reshape(cells_x * cells_y * cells_z)
    halo = jnp.concatenate([around, jnp.zeros((around.shape[0], 2, LANES), jnp.float32)], axis=1)
    embed, slope = call_pairs(0, dims, own, halo)
    slope_around = ghosts(slope.reshape(cells_x, cells_y, 1, cells_z * SLOTS))
    halo = jnp.concatenate([around, slope_around], axis=1)
    forces, energy = call_pairs(1, dims, own, halo, embed)
    return (
        forces.reshape(3, cells_x, cells_y, cells_z * SLOTS),
        energy.reshape(cells_x, cells_y, cells_z * SLOTS),
    )


def solution(mesh):
    return jax.shard_map(
        on_device,
        mesh=mesh,
        in_specs=(P(None, "gx", "gy", "gz"), P("gx", "gy", "gz")),
        out_specs=(P(None, "gx", "gy", "gz"), P("gx", "gy", "gz")),
        check_vma=False,
    )
```

time: 216 us -> 138 us (0.64)
  other arithmetic: 179 us -> 0.36 us
  Pallas kernels: 0 us -> 103 us
  local copies, waits for them, and re-layouts: 8.04 us -> 1.99 us
  waiting for transfers between devices: 10.8 us -> 13.9 us
    reduce_sum x22 -> x0, other arithmetic: 176 us -> none  [the longest x13 135 us: cell_forces(): jnp.sum(factor * displace[component], axis=-1)]
    pallas_call x0 -> x2, Pallas kernels: none -> 103 us  [call_pairs(): pl.pallas_call(functools.partial(pair_kernel, kind, dims), out_shape=outs...]
    reduce_sum x60 -> x0, local copies, waits for them, and re-layouts: 5.18 us -> none  [the longest x30 2.59 us: cell_forces(): jnp.sum(factor * displace[component], axis=-1)]
    ppermute x12, waiting for transfers between devices: 10.8 us -> 13.9 us  [the longest x6 9.9 us: swap(): before = lax.ppermute(high, axis, up)]
where the time goes in v1:
time: 138 us; the launch traced here: 137 us
  Pallas kernels  103 us (75%)
  starting transfers between devices  16.8 us (12%)
  waiting for transfers between devices  13.9 us (10%)
  local copies, waits for them, and re-layouts  1.99 us (1%)
    pallas_call x2, Pallas kernels, call_pairs(): pl.pallas_call(functools.partial(pair_kernel, kind, dims), out_shape=outs...  103 us
    ppermute x6, starting transfers between devices, swap(): after = lax.ppermute(low, axis, down)  10.4 us
    ppermute x6, waiting for transfers between devices, swap(): before = lax.ppermute(high, axis, up)  9.9 us
    ppermute x6, starting transfers between devices, swap(): before = lax.ppermute(high, axis, up)  6.34 us
    ppermute x6, waiting for transfers between devices, swap(): after = lax.ppermute(low, axis, down)  4.02 us
  transfers between devices with their start and end apart: 12, of which 10 were waited for; matrix products, arithmetic and copies ran while one was open for 0% of the time, Pallas kernels for 0%

profile of v1, /device:TPU:0, one launch (start us, length us, event | category | flops | bytes accessed | tf_op | source)
XLA Modules:
  0.0 136.9 jit_solution(17802758038264813891)
XLA Ops:
  0.6 0.1 iota.12
  0.7 0.8 copy.8
  1.5 0.0 copy-start
  1.5 0.1 lt.14
  1.6 0.1 lt.15
  1.7 0.6 copy-done
  2.3 0.1 fusion
  2.3 2.4 %collective-permute-start = (f32[4,4,3,64]{3,1,0,2:T(4,128)S(1)}, f32[4,4,3,64]{3,1,0,2:T(4,128)S(1)}, u32[]{:S(2)}, u32[]{:S(2)}) collective-permute-start(f32[4,4,3,64]{3,1,0,2:T(4,128)S(1)} %get-tuple-element.18), channel_id=1, source_target_pairs={{1,0},{2,1},{3,2},{0,3},{5,4},{6,5},{7,6},{4,7},{9,8},{10,9},{11,1... | collective-permute-start | bytes 36872 | tf_op jit(solution)/shard_map/ppermute | solution.py:320
  4.8 0.0 collective-permute-start.1
  4.8 1.6 %collective-permute-done = f32[4,4,3,64]{3,1,0,2:T(4,128)S(1)} collective-permute-done((f32[4,4,3,64]{3,1,0,2:T(4,128)S(1)}, f32[4,4,3,64]{3,1,0,2:T(4,128)S(1)}, u32[]{:S(2)}, u32[]{:S(2)}) %collective-permute-start) | collective-permute-done | bytes 12320 | tf_op jit(solution)/shard_map/ppermute | solution.py:320
  6.3 1.7 %collective-permute-done.1 = f32[4,4,3,64]{3,1,0,2:T(4,128)S(1)} collective-permute-done((f32[4,4,3,64]{3,1,0,2:T(4,128)S(1)}, f32[4,4,3,64]{3,1,0,2:T(4,128)S(1)}, u32[]{:S(2)}, u32[]{:S(2)}) %collective-permute-start.1) | collective-permute-done | bytes 12320 | tf_op jit(solution)/shard_map/ppermute | solution.py:319
  8.0 0.1 maximum_bitcast_fusion
  8.1 1.6 %collective-permute-start.2 = (f32[1,4,3,2,128]{4,1,0,2,3:T(4,128)S(1)}, f32[1,4,3,2,128]{4,1,0,2,3:T(4,128)S(1)}, u32[]{:S(2)}, u32[]{:S(2)}) collective-permute-start(f32[1,4,3,2,128]{4,1,0,2,3:T(4,128)S(1)} %get-tuple-element.12), channel_id=1, source_target_pairs={{0,8},{8,16},{16,24},{24,0},{1,9},{9,17},{17,25},{25,1},{2,10},{10... | collective-permute-start | bytes 36872 | tf_op jit(solution)/shard_map/ppermute | solution.py:319
  9.7 2.2 %collective-permute-start.3 = (f32[1,4,3,2,128]{4,1,0,2,3:T(4,128)S(1)}, f32[1,4,3,2,128]{4,1,0,2,3:T(4,128)S(1)}, u32[]{:S(2)}, u32[]{:S(2)}) collective-permute-start(f32[1,4,3,2,128]{4,1,0,2,3:T(4,128)S(1)} %get-tuple-element.13), channel_id=1, source_target_pairs={{8,0},{16,8},{24,16},{0,24},{9,1},{17,9},{25,17},{1,25},{10,2},{18... | collective-permute-start | bytes 36872 | tf_op jit(solution)/shard_map/ppermute | solution.py:320
  12.0 1.7 %collective-permute-done.2 = f32[1,4,3,2,128]{4,1,0,2,3:T(4,128)S(1)} collective-permute-done((f32[1,4,3,2,128]{4,1,0,2,3:T(4,128)S(1)}, f32[1,4,3,2,128]{4,1,0,2,3:T(4,128)S(1)}, u32[]{:S(2)}, u32[]{:S(2)}) %collective-permute-start.2) | collective-permute-done | bytes 12320 | tf_op jit(solution)/shard_map/ppermute | solution.py:319
  13.6 0.0 collective-permute-done.3
  13.7 1.6 %collective-permute-start.4 = (f32[6,1,3,2,128]{4,1,0,2,3:T(1,128)S(1)}, f32[6,1,3,2,128]{4,1,0,2,3:T(1,128)S(1)}, u32[]{:S(2)}, u32[]{:S(2)}) collective-permute-start(f32[6,1,3,2,128]{4,1,0,2,3:T(1,128)S(1)} %get-tuple-element.10), channel_id=1, source_target_pairs={{0,4},{4,0},{1,5},{5,1},{2,6},{6,2},{3,7},{7,3},{8,12},{12,8},{9,1... | collective-permute-start | bytes 55304 | tf_op jit(solution)/shard_map/ppermute | solution.py:319
  15.3 0.5 collective-permute-start.5
  15.8 0.1 reshape.32.refs_0_
  15.9 1.6 %collective-permute-done.4 = f32[6,1,3,2,128]{4,1,0,2,3:T(1,128)S(1)} collective-permute-done((f32[6,1,3,2,128]{4,1,0,2,3:T(1,128)S(1)}, f32[6,1,3,2,128]{4,1,0,2,3:T(1,128)S(1)}, u32[]{:S(2)}, u32[]{:S(2)}) %collective-permute-start.4) | collective-permute-done | bytes 18464 | tf_op jit(solution)/shard_map/ppermute | solution.py:319
  17.5 1.5 %collective-permute-done.5 = f32[6,1,3,2,128]{4,1,0,2,3:T(1,128)S(1)} collective-permute-done((f32[6,1,3,2,128]{4,1,0,2,3:T(1,128)S(1)}, f32[6,1,3,2,128]{4,1,0,2,3:T(1,128)S(1)}, u32[]{:S(2)}, u32[]{:S(2)}) %collective-permute-start.5) | collective-permute-done | bytes 18464 | tf_op jit(solution)/shard_map/ppermute | solution.py:320
  19.0 0.1 pad_maximum_fusion
  19.1 0.1 copy.10
  19.2 0.1 reshape.33
  19.3 45.8 %density.1 = (f32[16,128]{1,0:T(8,128)S(1)}, f32[16,128]{1,0:T(8,128)S(1)}) custom-call(s32[32]{0:T(128)S(1)} %reshape.32.refs_0_, f32[36,8,128]{2,1,0:T(8,128)S(1)} %concatenate.27.refs_1_), custom_call_target="tpu_custom_call" | custom-call | tf_op jit(solution)/shard_map/density/pallas_call | solution.py:296
  65.1 0.1 fusion.1
  65.2 0.0 collective-permute-start.6
  65.2 0.5 collective-permute-start.7
  65.7 0.9 collective-permute-done.6
  66.5 1.8 %collective-permute-done.7 = f32[4,4,1,64]{3,1,0,2:T(4,128)S(1)} collective-permute-done((f32[4,4,1,64]{3,1,0,2:T(4,128)S(1)}, f32[4,4,1,64]{3,1,0,2:T(4,128)S(1)}, u32[]{:S(2)}, u32[]{:S(2)}) %collective-permute-start.7) | collective-permute-done | bytes 4128 | tf_op jit(solution)/shard_map/ppermute | solution.py:319
  68.3 0.1 pad_maximum_fusion.9
  68.4 2.6 %collective-permute-start.8 = (f32[1,4,1,2,128]{4,3,1,0,2:T(2,128)S(1)}, f32[1,4,1,2,128]{4,3,1,0,2:T(2,128)S(1)}, u32[]{:S(2)}, u32[]{:S(2)}) collective-permute-start(f32[1,4,1,2,128]{4,3,1,0,2:T(2,128)S(1)} %get-tuple-element.20), channel_id=1, source_target_pairs={{0,8},{8,16},{16,24},{24,0},{1,9},{9,17},{17,25},{25,1},{2,10},{10... | collective-permute-start | bytes 12296 | tf_op jit(solution)/shard_map/ppermute | solution.py:319
  71.0 3.3 %collective-permute-start.9 = (f32[1,4,1,2,128]{4,3,1,0,2:T(2,128)S(1)}, f32[1,4,1,2,128]{4,3,1,0,2:T(2,128)S(1)}, u32[]{:S(2)}, u32[]{:S(2)}) collective-permute-start(f32[1,4,1,2,128]{4,3,1,0,2:T(2,128)S(1)} %get-tuple-element.21), channel_id=1, source_target_pairs={{8,0},{16,8},{24,16},{0,24},{9,1},{17,9},{25,17},{1,25},{10,2},{18... | collective-permute-start | bytes 12296 | tf_op jit(solution)/shard_map/ppermute | solution.py:320
  74.2 1.5 %collective-permute-done.8 = f32[1,4,1,2,128]{4,3,1,0,2:T(2,128)S(1)} collective-permute-done((f32[1,4,1,2,128]{4,3,1,0,2:T(2,128)S(1)}, f32[1,4,1,2,128]{4,3,1,0,2:T(2,128)S(1)}, u32[]{:S(2)}, u32[]{:S(2)}) %collective-permute-start.8) | collective-permute-done | bytes 4128 | tf_op jit(solution)/shard_map/ppermute | solution.py:319
  75.8 0.0 collective-permute-done.9
  75.8 0.1 collective-permute-start.10
  75.8 2.0 %collective-permute-start.11 = (f32[6,1,1,2,128]{4,3,1,0,2:T(2,128)S(1)}, f32[6,1,1,2,128]{4,3,1,0,2:T(2,128)S(1)}, u32[]{:S(2)}, u32[]{:S(2)}) collective-permute-start(f32[6,1,1,2,128]{4,3,1,0,2:T(2,128)S(1)} %get-tuple-element.17), channel_id=1, source_target_pairs={{4,0},{0,4},{5,1},{1,5},{6,2},{2,6},{7,3},{3,7},{12,8},{8,12},{13,... | collective-permute-start | bytes 18440 | tf_op jit(solution)/shard_map/ppermute | solution.py:320
  77.9 1.6 %collective-permute-done.10 = f32[6,1,1,2,128]{4,3,1,0,2:T(2,128)S(1)} collective-permute-done((f32[6,1,1,2,128]{4,3,1,0,2:T(2,128)S(1)}, f32[6,1,1,2,128]{4,3,1,0,2:T(2,128)S(1)}, u32[]{:S(2)}, u32[]{:S(2)}) %collective-permute-start.10) | collective-permute-done | bytes 6176 | tf_op jit(solution)/shard_map/ppermute | solution.py:319
  79.5 0.1 collective-permute-done.11
  79.6 57.3 %forces.1 = (f32[3,16,128]{2,1,0:T(8,128)}, f32[16,128]{1,0:T(8,128)}) custom-call(s32[32]{0:T(128)S(1)} %reshape.32.refs_0_, f32[36,8,128]{2,1,0:T(8,128)S(1)} %pad_maximum_fusion.1.refs_1_, f32[16,128]{1,0:T(8,128)S(1)} %get-tuple-element.7.refs_2_), custom_call_target="tpu_custom_call" | custom-call | tf_op jit(solution)/shard_map/forces/pallas_call | solution.py:296
  (10 shorter events, 0.2 us)
Async XLA Ops:
  1.5 0.7 copy-start
  2.3 4.0 %collective-permute-start = (f32[4,4,3,64]{3,1,0,2:T(4,128)S(1)}, f32[4,4,3,64]{3,1,0,2:T(4,128)S(1)}, u32[]{:S(2)}, u32[]{:S(2)}) collective-permute-start(f32[4,4,3,64]{3,1,0,2:T(4,128)S(1)} %get-tuple-element.18), channel_id=1, source_target_pairs={{1,0},{2,1},{3,2},{0,3},{5,4},{6,5},{7,6},{4,7},{9,8},{10,9},{11,1... | collective-permute-start | bytes 36872 | tf_op jit(solution)/shard_map/ppermute | solution.py:320
  4.8 3.3 %collective-permute-start.1 = (f32[4,4,3,64]{3,1,0,2:T(4,128)S(1)}, f32[4,4,3,64]{3,1,0,2:T(4,128)S(1)}, u32[]{:S(2)}, u32[]{:S(2)}) collective-permute-start(f32[4,4,3,64]{3,1,0,2:T(4,128)S(1)} %get-tuple-element.19), channel_id=1, source_target_pairs={{0,1},{1,2},{2,3},{3,0},{4,5},{5,6},{6,7},{7,4},{8,9},{9,10},{10,1... | collective-permute-start | bytes 36872 | tf_op jit(solution)/shard_map/ppermute | solution.py:319
  8.1 5.5 %collective-permute-start.2 = (f32[1,4,3,2,128]{4,1,0,2,3:T(4,128)S(1)}, f32[1,4,3,2,128]{4,1,0,2,3:T(4,128)S(1)}, u32[]{:S(2)}, u32[]{:S(2)}) collective-permute-start(f32[1,4,3,2,128]{4,1,0,2,3:T(4,128)S(1)} %get-tuple-element.12), channel_id=1, source_target_pairs={{0,8},{8,16},{16,24},{24,0},{1,9},{9,17},{17,25},{25,1},{2,10},{10... | collective-permute-start | bytes 36872 | tf_op jit(solution)/shard_map/ppermute | solution.py:319
  9.7 3.9 %collective-permute-start.3 = (f32[1,4,3,2,128]{4,1,0,2,3:T(4,128)S(1)}, f32[1,4,3,2,128]{4,1,0,2,3:T(4,128)S(1)}, u32[]{:S(2)}, u32[]{:S(2)}) collective-permute-start(f32[1,4,3,2,128]{4,1,0,2,3:T(4,128)S(1)} %get-tuple-element.13), channel_id=1, source_target_pairs={{8,0},{16,8},{24,16},{0,24},{9,1},{17,9},{25,17},{1,25},{10,2},{18... | collective-permute-start | bytes 36872 | tf_op jit(solution)/shard_map/ppermute | solution.py:320
  13.7 3.8 %collective-permute-start.4 = (f32[6,1,3,2,128]{4,1,0,2,3:T(1,128)S(1)}, f32[6,1,3,2,128]{4,1,0,2,3:T(1,128)S(1)}, u32[]{:S(2)}, u32[]{:S(2)}) collective-permute-start(f32[6,1,3,2,128]{4,1,0,2,3:T(1,128)S(1)} %get-tuple-element.10), channel_id=1, source_target_pairs={{0,4},{4,0},{1,5},{5,1},{2,6},{6,2},{3,7},{7,3},{8,12},{12,8},{9,1... | collective-permute-start | bytes 55304 | tf_op jit(solution)/shard_map/ppermute | solution.py:319
  15.3 3.8 %collective-permute-start.5 = (f32[6,1,3,2,128]{4,1,0,2,3:T(1,128)S(1)}, f32[6,1,3,2,128]{4,1,0,2,3:T(1,128)S(1)}, u32[]{:S(2)}, u32[]{:S(2)}) collective-permute-start(f32[6,1,3,2,128]{4,1,0,2,3:T(1,128)S(1)} %get-tuple-element.11), channel_id=1, source_target_pairs={{4,0},{0,4},{5,1},{1,5},{6,2},{2,6},{7,3},{3,7},{12,8},{8,12},{13,... | collective-permute-start | bytes 55304 | tf_op jit(solution)/shard_map/ppermute | solution.py:320
  65.2 1.4 %collective-permute-start.6 = (f32[4,4,1,64]{3,1,0,2:T(4,128)S(1)}, f32[4,4,1,64]{3,1,0,2:T(4,128)S(1)}, u32[]{:S(2)}, u32[]{:S(2)}) collective-permute-start(f32[4,4,1,64]{3,1,0,2:T(4,128)S(1)} %get-tuple-element.22), channel_id=1, source_target_pairs={{1,0},{2,1},{3,2},{0,3},{5,4},{6,5},{7,6},{4,7},{9,8},{10,9},{11,1... | collective-permute-start | bytes 12296 | tf_op jit(solution)/shard_map/ppermute | solution.py:320
  65.2 3.1 %collective-permute-start.7 = (f32[4,4,1,64]{3,1,0,2:T(4,128)S(1)}, f32[4,4,1,64]{3,1,0,2:T(4,128)S(1)}, u32[]{:S(2)}, u32[]{:S(2)}) collective-permute-start(f32[4,4,1,64]{3,1,0,2:T(4,128)S(1)} %get-tuple-element.23), channel_id=1, source_target_pairs={{0,1},{1,2},{2,3},{3,0},{4,5},{5,6},{6,7},{7,4},{8,9},{9,10},{10,1... | collective-permute-start | bytes 12296 | tf_op jit(solution)/shard_map/ppermute | solution.py:319
  68.4 7.3 %collective-permute-start.8 = (f32[1,4,1,2,128]{4,3,1,0,2:T(2,128)S(1)}, f32[1,4,1,2,128]{4,3,1,0,2:T(2,128)S(1)}, u32[]{:S(2)}, u32[]{:S(2)}) collective-permute-start(f32[1,4,1,2,128]{4,3,1,0,2:T(2,128)S(1)} %get-tuple-element.20), channel_id=1, source_target_pairs={{0,8},{8,16},{16,24},{24,0},{1,9},{9,17},{17,25},{25,1},{2,10},{10... | collective-permute-start | bytes 12296 | tf_op jit(solution)/shard_map/ppermute | solution.py:319
  71.0 4.8 %collective-permute-start.9 = (f32[1,4,1,2,128]{4,3,1,0,2:T(2,128)S(1)}, f32[1,4,1,2,128]{4,3,1,0,2:T(2,128)S(1)}, u32[]{:S(2)}, u32[]{:S(2)}) collective-permute-start(f32[1,4,1,2,128]{4,3,1,0,2:T(2,128)S(1)} %get-tuple-element.21), channel_id=1, source_target_pairs={{8,0},{16,8},{24,16},{0,24},{9,1},{17,9},{25,17},{1,25},{10,2},{18... | collective-permute-start | bytes 12296 | tf_op jit(solution)/shard_map/ppermute | solution.py:320
  75.8 3.7 %collective-permute-start.10 = (f32[6,1,1,2,128]{4,3,1,0,2:T(2,128)S(1)}, f32[6,1,1,2,128]{4,3,1,0,2:T(2,128)S(1)}, u32[]{:S(2)}, u32[]{:S(2)}) collective-permute-start(f32[6,1,1,2,128]{4,3,1,0,2:T(2,128)S(1)} %get-tuple-element.16), channel_id=1, source_target_pairs={{0,4},{4,0},{1,5},{5,1},{2,6},{6,2},{3,7},{7,3},{8,12},{12,8},{9,1... | collective-permute-start | bytes 18440 | tf_op jit(solution)/shard_map/ppermute | solution.py:319
  75.8 3.7 %collective-permute-start.11 = (f32[6,1,1,2,128]{4,3,1,0,2:T(2,128)S(1)}, f32[6,1,1,2,128]{4,3,1,0,2:T(2,128)S(1)}, u32[]{:S(2)}, u32[]{:S(2)}) collective-permute-start(f32[6,1,1,2,128]{4,3,1,0,2:T(2,128)S(1)} %get-tuple-element.17), channel_id=1, source_target_pairs={{4,0},{0,4},{5,1},{1,5},{6,2},{2,6},{7,3},{3,7},{12,8},{8,12},{13,... | collective-permute-start | bytes 18440 | tf_op jit(solution)/shard_map/ppermute | solution.py:320

commit v2 on v1

v2 whole, which is shorter than its diff:
```python
import functools
import math

import jax
import jax.numpy as jnp
from jax import lax
from jax.experimental import pallas as pl
from jax.experimental.pallas import tpu as pltpu
from jax.sharding import PartitionSpec as P

SLOTS = 64
LANES = 128
FAR = 1.0e4

lattice_const = 3.615
cell_span = (2.0 * lattice_const, 2.0 * lattice_const, 4.0 * lattice_const)
cut_radius = 5.50679
cut_width = 0.50037
dens_scale = 3.80362
beta_one = 0.17394
radius_three = -2.19885
energy_one = 201.458
energy_two = 0.00659288
radius_one = 0.83591
radius_two = 4.46867
alpha_one = 2.97758
alpha_two = 1.54927
shift_delta = 0.0086225
repulsion = ((4.0, 2.24), (40.0, 1.8), (1150.0, 1.2))
embed_zero = -2.28235
embed_curve = 1.35535
lower_terms = (-1.27775, -0.86074, 1.78804, 2.97571)
upper_quartic = 0.4
upper_damping = 0.3
LOG2E = math.log2(math.e)
KEEP_SQUARED = 5.5075**2
ROWS = 16
WIDE = 2
TILES = 20


def embedding(density):
    excess = density - 1.0
    square = excess * excess
    cube = square * excess
    below_value = embed_zero + square * (
        0.5 * embed_curve
        + excess
        * (lower_terms[0] + excess * (lower_terms[1] + excess * (lower_terms[2] + excess * lower_terms[3])))
    )
    below_slope = excess * (
        embed_curve
        + excess
        * (
            3.0 * lower_terms[0]
            + excess * (4.0 * lower_terms[1] + excess * (5.0 * lower_terms[2] + excess * 6.0 * lower_terms[3]))
        )
    )
    numerator = embed_zero + square * (0.5 * embed_curve + excess * (lower_terms[0] + excess * upper_quartic))
    numer_slope = excess * (embed_curve + excess * (3.0 * lower_terms[0] + excess * 4.0 * upper_quartic))
    is_below = excess < 0.0
    denominator = jnp.where(is_below, 1.0, 1.0 + upper_damping * cube)
    above_value = numerator / denominator
    above_slope = (numer_slope - above_value * (3.0 * upper_damping) * square) / denominator
    return (
        jnp.where(is_below, below_value, above_value),
        jnp.where(is_below, below_slope, above_slope),
    )


def iota(shape, dim):
    return lax.broadcasted_iota(jnp.int32, shape, dim)


def compress_cells(halo_ref, cx, cy, ny):
    shape = (8, LANES)
    row = iota(shape, 0)
    lane = iota(shape, 1)
    comp = row // 2
    odd = row % 2
    layer = jnp.where(odd == 0, jnp.where(lane < SLOTS, 0, 1), jnp.where(lane < SLOTS, 2, -1))
    is_x, is_y, is_z = (comp == 0, comp == 1, comp == 2)
    span = jnp.where(is_z, cell_span[2], jnp.where(is_y, cell_span[1], cell_span[0]))
    counted = comp < 3
    pre = jnp.where(iota((LANES, 2 * LANES), 1) >= LANES, 1.0, 0.0)
    pre = jnp.where(iota((LANES, 2 * LANES), 0) < iota((LANES, 2 * LANES), 1), 1.0, pre).astype(jnp.bfloat16)
    data, drops = ([], [])
    for cz in (0, 1):
        add_z = jnp.where(is_z, (layer - cz).astype(jnp.float32) * cell_span[2], 0.0)
        for o1 in (-1, 0, 1):
            for o2 in (-1, 0, 1):
                add = jnp.where(is_x, o1 * cell_span[0], jnp.where(is_y, o2 * cell_span[1], add_z))
                value = halo_ref[(cx + 1 + o1) * ny + cy + 1 + o2] + add
                gap = jnp.maximum(jnp.maximum(-value, value - span), 0.0)
                gap = jnp.where(counted, gap * gap, 0.0)
                gap = gap + pltpu.roll(gap, 4, 0)
                gap = gap + pltpu.roll(gap, 2, 0)
                data.append(value)
                drops.append(gap >= KEEP_SQUARED)
    dropped = jnp.concatenate([jnp.where(d, 1.0, 0.0) for d in drops], axis=0).astype(jnp.bfloat16)
    sums = jnp.dot(dropped, pre, preferred_element_type=jnp.float32).astype(jnp.int32)
    moves = [jnp.where(drops[k], 0, sums[8 * k : 8 * k + 8, :LANES]) for k in range(18)]
    for bit in range(7):
        step = 1 << bit
        for k in range(18):
            value_in = pltpu.roll(data[k], LANES - step, 1)
            move_in = pltpu.roll(moves[k], LANES - step, 1)
            comes = (move_in & step) != 0
            data[k] = jnp.where(comes, value_in, data[k])
            moves[k] = jnp.where(comes, move_in, jnp.where((moves[k] & step) != 0, 0, moves[k]))
    counts = []
    one_row = iota((1, LANES), 1)
    for cz in (0, 1):
        line = jnp.zeros((1, LANES), jnp.int32)
        for k in range(9):
            first = 8 * (9 * cz + k)
            total = LANES - sums[first : first + 8, LANES:]
            line = jnp.where(one_row == 2 * k, total[0:1], line)
            line = jnp.where(one_row == 2 * k + 1, total[1:2], line)
        counts.append(line)
    return data, counts


def merge_cells(packed_ref, count_ref, list_ref, column):
    lane = iota((8, LANES), 1)
    offset = [jnp.int32(0), jnp.int32(0)]
    current = [jnp.zeros((8, LANES), jnp.float32) for _ in range(2)]
    for k in range(18):
        for cz in (0, 1):
            cell = column * 2 + cz
            number = count_ref[cell, k]
            place = offset[cz] & (LANES - 1)
            turned = pltpu.roll(packed_ref[cell * 18 + k], place, 1)
            current[cz] = jnp.where(lane >= place, turned, current[cz])
            list_ref[cell * TILES + (offset[cz] >> 7)] = current[cz]
            current[cz] = jnp.where(lane < place + number - LANES, turned, current[cz])
            offset[cz] = offset[cz] + number
    for cz in (0, 1):
        first = (column * 2 + cz) * TILES + (offset[cz] >> 7)
        list_ref[first] = jnp.where(lane >= (offset[cz] & (LANES - 1)), FAR, current[cz])
        for extra in range(1, WIDE):
            list_ref[first + extra] = jnp.full((8, LANES), FAR, jnp.float32)
    return offset


def pair_parts(centers, tile, slopes=None):
    d = [tile[2 * c : 2 * c + 1] - centers[c] for c in range(3)]
    squared = d[0] * d[0] + d[1] * d[1] + d[2] * d[2]
    squared = jnp.where(squared < 0.25, 100.0, squared)
    inv = lax.rsqrt(squared)
    radius = squared * inv
    scaled = jnp.minimum(radius * (1.0 / cut_width) - cut_radius / cut_width, 0.0)
    square = scaled * scaled
    quartic = square * square
    inverse = pl.reciprocal(1.0 + quartic, approx=False)
    taper = quartic * inverse
    scale = math.sqrt(beta_one * LOG2E)
    along = radius * scale - radius_three * scale
    gauss = jnp.exp2(math.log2(dens_scale) - along * along)
    if slopes is None:
        return (gauss * taper,)
    taper_slope = (square * scaled) * (inverse * inverse) * (4.0 / cut_width)
    dens_slope = gauss * (taper_slope - (along * (2.0 * beta_one / scale)) * taper)
    u = jnp.exp2(radius * (-alpha_one * LOG2E) + alpha_one * LOG2E * radius_one)
    v = jnp.exp2(radius * (-alpha_two * LOG2E) + alpha_two * LOG2E * radius_two)
    a = u * u - u
    b = v * v - v
    base = energy_one * (a - u) + (energy_two * (b - v) + shift_delta)
    base_slope = (-2.0 * alpha_one * energy_one) * a + (-2.0 * alpha_two * energy_two) * b
    pair_slope = base_slope * taper + base * taper_slope
    quarter = None
    for strength, reach in repulsion:
        close = jnp.maximum(reach - radius, 0.0)
        cubed = (4.0 * strength) * (close * close * close)
        pair_slope = pair_slope + cubed
        quarter = cubed * close if quarter is None else quarter + cubed * close
    pair_value = base * taper - 0.25 * quarter
    factor = (pair_slope + slopes * dens_slope) * inv
    return pair_value, factor * d[0], factor * d[1], factor * d[2]


def fold(value):
    total = value[:, :LANES]
    for k in range(1, WIDE):
        total = total + value[:, k * LANES : (k + 1) * LANES]
    return total


def lane_sums(value):
    high = value.astype(jnp.bfloat16)
    low = (value - high.astype(jnp.float32)).astype(jnp.bfloat16)
    both = jnp.concatenate([high, low], axis=1)
    ones = jnp.ones((8, 2 * LANES), jnp.bfloat16)
    total = lax.dot_general(ones, both, (((1,), (1,)), ((), ())), preferred_element_type=jnp.float32)
    return total[0:1]


class Exchange:
    def __init__(self, sizes, own, ref, send, recv):
        self.sizes, self.own, self.ref, self.send, self.recv = sizes, own, ref, send, recv

    def copy(self, index, source, target, axis, shift):
        count = self.sizes[axis]
        peer = lax.rem(lax.axis_index(axis) + (shift + count), count)
        return pltpu.make_async_remote_copy(
            src_ref=source,
            dst_ref=target,
            send_sem=self.send.at[index],
            recv_sem=self.recv.at[index],
            device_id={axis: peer},
            device_id_type=pl.DeviceIdType.MESH,
        )

    def phases(self):
        ref = self.ref
        cx, cy = (ref.shape[0] - 2, ref.shape[1] - 2)
        inner = ref.at[pl.ds(1, cx), pl.ds(1, cy)]
        return (
            (
                self.copy(0, self.own, inner.at[:, :, 1], "gz", 1),
                self.copy(1, self.own, inner.at[:, :, 2], "gz", -1),
            ),
            (
                self.copy(2, ref.at[pl.ds(cx, 1), pl.ds(1, cy)], ref.at[pl.ds(0, 1), pl.ds(1, cy)], "gx", 1),
                self.copy(3, ref.at[pl.ds(1, 1), pl.ds(1, cy)], ref.at[pl.ds(cx + 1, 1), pl.ds(1, cy)], "gx", -1),
            ),
            (
                self.copy(4, ref.at[:, pl.ds(cy, 1)], ref.at[:, pl.ds(0, 1)], "gy", 1),
                self.copy(5, ref.at[:, pl.ds(1, 1)], ref.at[:, pl.ds(cy + 1, 1)], "gy", -1),
            ),
        )


def run_phase(copies, wait):
    for copy in copies:
        if wait:
            copy.wait()
        else:
            copy.start()


def exchange_kernel(sizes, own_ref, *refs):
    halo_ref, around_ref, sem, send_sem, recv_sem = refs[-5:]
    cells_x, cells_y, comps = own_ref.shape[:3]
    nx, ny = (cells_x + 2, cells_y + 2)
    barrier = pltpu.get_barrier_semaphore()
    for axis, count in sizes.items():
        for shift in (1, count - 1):
            peer = lax.rem(lax.axis_index(axis) + shift, count)
            pl.semaphore_signal(
                barrier, inc=1, device_id={axis: peer}, device_id_type=pl.DeviceIdType.MESH
            )
    keep = pltpu.make_async_copy(
        own_ref, around_ref.at[pl.ds(1, cells_x), pl.ds(1, cells_y), 0], sem
    )
    keep.start()
    pl.semaphore_wait(barrier, 2 * len(sizes))
    phases = Exchange(sizes, own_ref, around_ref, send_sem, recv_sem).phases()
    run_phase(phases[0], False)
    keep.wait()
    run_phase(phases[0], True)
    for copies in phases[1:]:
        run_phase(copies, False)
        run_phase(copies, True)

    lane_row = iota((1, LANES), 1)
    low_half = lane_row < SLOTS
    lanes = lane_row.astype(jnp.float32)
    for x in range(nx):
        for y in range(ny):
            rows = []
            for c in range(comps):
                rows.append(around_ref[x, y, 0, c : c + 1])
                rows.append(
                    jnp.where(low_half, around_ref[x, y, 2, c : c + 1], around_ref[x, y, 1, c : c + 1])
                )
            rows = rows + [lanes, lanes] if comps == 3 else rows * 4
            halo_ref[x * ny + y] = jnp.concatenate(rows, axis=0)


def call_exchange(sizes, own, number, held=()):
    cells_x, cells_y, comps = own.shape[:3]
    nx, ny = (cells_x + 2, cells_y + 2)
    vmem = pl.BlockSpec(memory_space=pltpu.VMEM)
    return pl.pallas_call(
        functools.partial(exchange_kernel, sizes),
        out_shape=jax.ShapeDtypeStruct((nx * ny, 8, LANES), jnp.float32),
        in_specs=[vmem] + [pl.BlockSpec(memory_space=pl.ANY)] * len(held),
        out_specs=vmem,
        scratch_shapes=[
            pltpu.VMEM((nx, ny, 3, comps, LANES), jnp.float32),
            pltpu.SemaphoreType.DMA,
            pltpu.SemaphoreType.DMA((6,)),
            pltpu.SemaphoreType.DMA((6,)),
        ],
        compiler_params=pltpu.CompilerParams(
            vmem_limit_bytes=8 * 1024 * 1024, collective_id=number, has_side_effects=True
        ),
        name="exchange",
    )(own, *held)


def density_kernel(
    own_ref,
    placed_ref,
    halo_ref,
    slope_ref,
    embed_ref,
    packed_ref,
    list_ref,
    center_ref,
    count_vmem,
    count_ref,
    length_ref,
    sum_ref,
    sem,
):
    cells_x, cells_y = placed_ref.shape[:2]
    columns = cells_x * cells_y
    ny = cells_y + 2

    @pl.loop(0, columns)
    def _(column):
        value = placed_ref[column // cells_y, column % cells_y]
        for c in range(3):
            center_ref[column, c] = jnp.transpose(jnp.broadcast_to(value[c : c + 1], (LANES, LANES)))

    @pl.loop(0, columns)
    def _(column):
        outs, counts = compress_cells(halo_ref, column // cells_y, column % cells_y, ny)
        for k in range(18):
            packed_ref[column * 36 + 2 * k] = outs[k]
            packed_ref[column * 36 + 2 * k + 1] = pltpu.roll(outs[k], 7, 0)
        for cz in (0, 1):
            count_vmem[pl.ds(column * 2 + cz, 1), :] = counts[cz]

    copy = pltpu.make_async_copy(count_vmem, count_ref, sem)
    copy.start()
    copy.wait()

    @pl.loop(0, columns)
    def _(column):
        lengths = merge_cells(packed_ref, count_ref, list_ref, column)
        for cz in (0, 1):
            length_ref[column * 2 + cz] = (lengths[cz] + (WIDE * LANES - 1)) >> int(math.log2(WIDE * LANES))

    @pl.loop(0, 2 * columns)
    def _(cell):
        column = cell // 2
        begin = (cell % 2) * SLOTS
        steps = length_ref[cell]
        blocks = (own_ref[cell] + ROWS - 1) // ROWS

        @pl.loop(0, blocks)
        def _(block):
            start = pl.multiple_of(begin + block * ROWS, ROWS)
            centers = [
                jnp.concatenate([center_ref[column, c, pl.ds(start, ROWS), :]] * WIDE, axis=1) for c in range(3)
            ]

            def step(index, sums):
                tile = jnp.concatenate(
                    [list_ref[cell * TILES + index * WIDE + k] for k in range(WIDE)], axis=1
                )
                return (sums[0] + fold(pair_parts(centers, tile)[0]),)

            zero = jnp.zeros((ROWS, LANES), jnp.float32)
            sums = lax.fori_loop(0, steps, step, (zero,))
            sum_ref[0, column, pl.ds(start, ROWS), :] = sums[0]

    filled = jnp.concatenate(
        [placed_ref[c // cells_y, c % cells_y, 0:1] for c in range(columns)], axis=0
    ) < 0.5 * FAR
    density = jnp.concatenate([lane_sums(sum_ref[0, c]) for c in range(columns)], axis=0)
    embed_value, embed_slope = embedding(jnp.where(filled, density, 0.0))
    slope = jnp.where(filled, embed_slope, 0.0)
    for c in range(columns):
        slope_ref[c // cells_y, c % cells_y] = slope[c : c + 1]
    embed_ref[...] = embed_value


def force_kernel(
    own_ref,
    placed_ref,
    slope_own,
    embed_ref,
    halo_ref,
    packed_in,
    list_ref,
    center_ref,
    count_vmem,
    force_ref,
    energy_ref,
    packed_ref,
    slope_list,
    slope_center,
    count_ref,
    length_ref,
    sum_ref,
    sem,
):
    cells_x, cells_y = placed_ref.shape[:2]
    columns = cells_x * cells_y
    ny = cells_y + 2
    copy = pltpu.make_async_copy(count_vmem, count_ref, sem)
    copy.start()
    filled = jnp.concatenate(
        [placed_ref[c // cells_y, c % cells_y, 0:1] for c in range(columns)], axis=0
    ) < 0.5 * FAR

    @pl.loop(0, columns)
    def _(column):
        value = slope_own[column // cells_y, column % cells_y]
        slope_center[column] = jnp.transpose(jnp.broadcast_to(value, (LANES, LANES)))

    @pl.loop(0, columns)
    def _(column):
        cx, cy = (column // cells_y, column % cells_y)
        for k in range(9):
            value = halo_ref[(cx + k // 3) * ny + cy + k % 3]
            for cz in (0, 1):
                at = column * 36 + 18 * cz + 2 * k
                index = packed_in[at].astype(jnp.int32) & (LANES - 1)
                taken = jnp.take_along_axis(value, index, axis=1, mode="promise_in_bounds")
                packed_ref[at] = taken
                packed_ref[at + 1] = pltpu.roll(taken, 7, 0)

    copy.wait()

    @pl.loop(0, columns)
    def _(column):
        lengths = merge_cells(packed_ref, count_ref, slope_list, column)
        for cz in (0, 1):
            length_ref[column * 2 + cz] = (lengths[cz] + (WIDE * LANES - 1)) >> int(math.log2(WIDE * LANES))

    @pl.loop(0, 2 * columns)
    def _(cell):
        column = cell // 2
        begin = (cell % 2) * SLOTS
        steps = length_ref[cell]
        blocks = (own_ref[cell] + ROWS - 1) // ROWS

        @pl.loop(0, blocks)
        def _(block):
            start = pl.multiple_of(begin + block * ROWS, ROWS)
            centers = [
                jnp.concatenate([center_ref[column, c, pl.ds(start, ROWS), :]] * WIDE, axis=1) for c in range(3)
            ]
            slope_i = jnp.concatenate([slope_center[column, pl.ds(start, ROWS), :]] * WIDE, axis=1)

            def step(index, sums):
                at = [cell * TILES + index * WIDE + k for k in range(WIDE)]
                tile = jnp.concatenate([list_ref[t] for t in at], axis=1)
                slope_j = jnp.concatenate([slope_list[t] for t in at], axis=1)[6:7]
                parts = pair_parts(centers, tile, slope_i + slope_j)
                return tuple(total + fold(part) for total, part in zip(sums, parts))

            zero = jnp.zeros((ROWS, LANES), jnp.float32)
            sums = lax.fori_loop(0, steps, step, (zero,) * 4)
            for k in range(4):
                sum_ref[k, column, pl.ds(start, ROWS), :] = sums[k]

    pair_sum = jnp.concatenate([lane_sums(sum_ref[0, c]) for c in range(columns)], axis=0)
    energy_ref[...] = jnp.where(filled, embed_ref[...] + 0.5 * pair_sum, 0.0)
    for k in range(3):
        total = jnp.concatenate([lane_sums(sum_ref[1 + k, c]) for c in range(columns)], axis=0)
        force_ref[k] = jnp.where(filled, total, 0.0)


def on_device(positions, counts):
    cells_x, cells_y, cells_z = counts.shape
    columns = cells_x * cells_y
    cells = columns * cells_z
    occupied = lax.broadcasted_iota(jnp.int32, (cells_x, cells_y, cells_z, SLOTS), 3) < counts[..., None]
    occupied = occupied.reshape(1, cells_x, cells_y, cells_z * SLOTS)
    placed = jnp.transpose(jnp.where(occupied, positions, FAR), (1, 2, 0, 3))
    sizes = {axis: lax.axis_size(axis) for axis in ("gx", "gy", "gz")}
    own = counts.reshape(cells)
    vmem = pl.BlockSpec(memory_space=pltpu.VMEM)
    smem = pl.BlockSpec(memory_space=pltpu.SMEM)
    f32 = jnp.float32
    shape = jax.ShapeDtypeStruct
    params = pltpu.CompilerParams(vmem_limit_bytes=24 * 1024 * 1024)
    halo = call_exchange(sizes, placed, 0)
    work = [
        pltpu.SMEM((cells, LANES), jnp.int32),
        pltpu.SMEM((cells,), jnp.int32),
        pltpu.VMEM((4, columns, LANES, LANES), f32),
        pltpu.SemaphoreType.DMA,
    ]
    saved = (
        shape((cells * 18, 8, LANES), f32),
        shape((cells * TILES, 8, LANES), f32),
        shape((columns, 3, LANES, LANES), f32),
        shape((cells, LANES), jnp.int32),
    )
    slope, embed, *kept = pl.pallas_call(
        density_kernel,
        out_shape=(shape((cells_x, cells_y, 1, LANES), f32), shape((columns, LANES), f32)) + saved,
        in_specs=[smem, vmem, vmem],
        out_specs=(vmem,) * 6,
        scratch_shapes=work,
        compiler_params=params,
        name="density",
    )(own, placed, halo)
    halo = call_exchange(sizes, slope, 1)
    forces, energy = pl.pallas_call(
        force_kernel,
        out_shape=(shape((3, columns, LANES), f32), shape((columns, LANES), f32)),
        in_specs=[smem] + [vmem] * 8,
        out_specs=(vmem, vmem),
        scratch_shapes=[
            pltpu.VMEM((cells * 18, 8, LANES), f32),
            pltpu.VMEM((cells * TILES, 8, LANES), f32),
            pltpu.VMEM((columns, LANES, LANES), f32),
        ]
        + work,
        compiler_params=params,
        name="forces",
    )(own, placed, slope, embed, halo, *kept)
    return (
        forces.reshape(3, cells_x, cells_y, cells_z * SLOTS),
        energy.reshape(cells_x, cells_y, cells_z * SLOTS),
    )


def solution(mesh):
    return jax.shard_map(
        on_device,
        mesh=mesh,
        in_specs=(P(None, "gx", "gy", "gz"), P("gx", "gy", "gz")),
        out_specs=(P(None, "gx", "gy", "gz"), P("gx", "gy", "gz")),
        check_vma=False,
    )
```

time: 138 us -> 74.7 us (0.54)
  Pallas kernels: 103 us -> 71.4 us
  starting transfers between devices: 16.8 us -> 0 us
  waiting for transfers between devices: 13.9 us -> 0 us
    pallas_call x2 -> x4, Pallas kernels: 103 us -> 71.4 us  [the longest x1 24.7 us: on_device(): pl.pallas_call(density_kernel, out_shape=(shape((cells_x, cells_y, 1, LAN...]
    ppermute x12 -> x0, starting transfers between devices: 16.8 us -> none  [the longest x6 10.4 us: swap(): after = lax.ppermute(low, axis, down)]
    ppermute x12 -> x0, waiting for transfers between devices: 13.9 us -> none  [the longest x6 9.9 us: swap(): before = lax.ppermute(high, axis, up)]
  transfers between devices with their start and end apart: 12 -> 0, of which waited for: 10 -> 0; matrix products, arithmetic and copies ran while one was open for 0% -> 0% of each run, Pallas kernels for 0% -> 0%
where the time goes in v2:
time: 74.7 us; the launch traced here: 73.9 us
  Pallas kernels  71.4 us (96%)
  local copies, waits for them, and re-layouts  1.14 us (2%)
  other arithmetic  0.77 us (1%)
    pallas_call x1, Pallas kernels, on_device(): pl.pallas_call(density_kernel, out_shape=(shape((cells_x, cells_y, 1, LAN...  24.7 us
    pallas_call x2, Pallas kernels, call_exchange(): pl.pallas_call(functools.partial(exchange_kernel, sizes), out_shape=jax.S...  24.5 us
    pallas_call x1, Pallas kernels, on_device(): pl.pallas_call(force_kernel, out_shape=(shape((3, columns, LANES), f32),...  22.2 us

profile of v2, /device:TPU:0, one launch (start us, length us, event | category | flops | bytes accessed | tf_op | source)
XLA Modules:
  0.0 73.9 jit_solution(3032390811156761701)
XLA Ops:
  0.6 0.1 iota.12
  0.7 0.8 %copy.7 = s32[4,4,2]{2,1,0:T(4,128)S(1)} copy(s32[4,4,2]{1,2,0:T(2,128)} %param.3) | data formatting | bytes 256 | tf_op args[1]
  1.5 0.1 reshape.23.own_ref
  1.6 0.1 lt.14
  1.7 0.1 lt.15
  1.8 0.8 %fusion.own_ref.placed_ref = f32[4,4,3,128]{3,2,1,0:T(4,128)S(1)} fusion(f32[3,4,4,128]{3,2,1,0:T(4,128)} %param.2, pred[4,4,128]{2,1,0:T(4,128)(4,1)S(1)} %broadcast_compare_fusion), kind=kLoop, calls=%fused_computation.1 | loop fusion | flops 6144 | bytes 51200 | tf_op jit(solution)/shard_map/transpose | solution.py:476
  2.6 14.0 %exchange.2.halo_ref = f32[36,8,128]{2,1,0:T(8,128)S(1)} custom-call(f32[4,4,3,128]{3,2,1,0:T(4,128)S(1)} %fusion.own_ref.placed_ref), custom_call_target="tpu_custom_call" | custom-call | tf_op jit(solution)/shard_map/exchange/pallas_call | solution.py:285
  16.6 24.7 %density.1 = (f32[4,4,1,128]{3,2,1,0:T(1,128)S(1)}, f32[16,128]{1,0:T(8,128)S(1)}, f32[576,8,128]{2,1,0:T(8,128)S(1)}, f32[640,8,128]{2,1,0:T(8,128)S(1)}, f32[1...) custom-call(s32[32]{0:T(128)S(1)} %reshape.23.own_ref, f32[4,4,3,128]{3,2,1,0:T(4,128)S(1)} %fusion.own_ref.placed_ref, ...), custom_call_target="tpu_custom_call" | custom-call | tf_op jit(solution)/shard_map/density/pallas_call | solution.py:497
  41.3 10.4 %exchange.3.halo_ref = f32[36,8,128]{2,1,0:T(8,128)S(1)} custom-call(f32[4,4,1,128]{3,2,1,0:T(1,128)S(1)} %get-tuple-element.10.own_ref.slope_own), custom_call_target="tpu_custom_call" | custom-call | tf_op jit(solution)/shard_map/exchange/pallas_call | solution.py:285
  51.7 22.2 %forces.1 = (f32[3,16,128]{2,1,0:T(8,128)}, f32[16,128]{1,0:T(8,128)}) custom-call(s32[32]{0:T(128)S(1)} %reshape.23.own_ref, f32[4,4,3,128]{3,2,1,0:T(4,128)S(1)} %fusion.own_ref.placed_ref, f32[4,4,1,128]{3,2,1,0:T(1,128)S(1)} %get-tuple-element.10.own_ref.slope_own, f32[16,128]{1,0:T(8,128)S(1)} %get-tuple-element.11.embed_ref, ...), custom_call_target="tpu_custom_call" | custom-call | tf_op jit(solution)/shard_map/forces/pallas_call | solution.py:507
  (2 shorter events, 0.0 us)

commit v3 on v2

--- a/solution.py
+++ b/solution.py
@@ -97,24 +97,38 @@
                 gap = gap + pltpu.roll(gap, 2, 0)
                 data.append(value)
                 drops.append(gap >= KEEP_SQUARED)
-    dropped = jnp.concatenate([jnp.where(d, 1.0, 0.0) for d in drops], axis=0).astype(jnp.bfloat16)
-    sums = jnp.dot(dropped, pre, preferred_element_type=jnp.float32).astype(jnp.int32)
-    moves = [jnp.where(drops[k], 0, sums[8 * k : 8 * k + 8, :LANES]) for k in range(18)]
+    dropped = [jnp.where(d, 1.0, 0.0) for d in drops]
+    groups = []
+    for first in range(0, 18, 4):
+        merged = dropped[first]
+        for k in range(first + 1, min(first + 4, 18)):
+            merged = jnp.where(comp == k - first, dropped[k], merged)
+        groups.append(merged)
+    sums = jnp.dot(
+        jnp.concatenate(groups, axis=0).astype(jnp.bfloat16), pre, preferred_element_type=jnp.float32
+    ).astype(jnp.int32)
+    moves = [
+        jnp.where(g > 0.5, 0, sums[8 * n : 8 * n + 8, :LANES]) for n, g in enumerate(groups)
+    ]
     for bit in range(7):
         step = 1 << bit
-        for k in range(18):
-            value_in = pltpu.roll(data[k], LANES - step, 1)
-            move_in = pltpu.roll(moves[k], LANES - step, 1)
-            comes = (move_in & step) != 0
-            data[k] = jnp.where(comes, value_in, data[k])
-            moves[k] = jnp.where(comes, move_in, jnp.where((moves[k] & step) != 0, 0, moves[k]))
+        for n in range(len(moves)):
+            move_in = pltpu.roll(moves[n], LANES - step, 1)
+            stay = jnp.where((moves[n] & step) != 0, 0, moves[n])
+            moves[n] = jnp.where((move_in & step) != 0, move_in, stay)
+    indices = [lane + move for move in moves]
+    for k in range(18):
+        index = jnp.where(comp == k % 4, indices[k // 4], 0)
+        index = index + pltpu.roll(index, 4, 0)
+        index = index + pltpu.roll(index, 2, 0)
+        data[k] = jnp.take_along_axis(data[k], index & (LANES - 1), axis=1, mode="promise_in_bounds")
     counts = []
     one_row = iota((1, LANES), 1)
     for cz in (0, 1):
         line = jnp.zeros((1, LANES), jnp.int32)
         for k in range(9):
-            first = 8 * (9 * cz + k)
-            total = LANES - sums[first : first + 8, LANES:]
+            first = 2 * (9 * cz + k)
+            total = LANES - sums[first : first + 2, LANES:]
             line = jnp.where(one_row == 2 * k, total[0:1], line)
             line = jnp.where(one_row == 2 * k + 1, total[1:2], line)
         counts.append(line)
@@ -152,7 +166,9 @@
     scaled = jnp.minimum(radius * (1.0 / cut_width) - cut_radius / cut_width, 0.0)
     square = scaled * scaled
     quartic = square * square
-    inverse = pl.reciprocal(1.0 + quartic, approx=False)
+    bottom = 1.0 + quartic
+    inverse = pl.reciprocal(bottom, approx=True)
+    inverse = inverse * (2.0 - bottom * inverse)
     taper = quartic * inverse
     scale = math.sqrt(beta_one * LOG2E)
     along = radius * scale - radius_three * scale
@@ -195,73 +211,49 @@
     return total[0:1]
 
 
-class Exchange:
-    def __init__(self, sizes, own, ref, send, recv):
-        self.sizes, self.own, self.ref, self.send, self.recv = sizes, own, ref, send, recv
-
-    def copy(self, index, source, target, axis, shift):
-        count = self.sizes[axis]
-        peer = lax.rem(lax.axis_index(axis) + (shift + count), count)
-        return pltpu.make_async_remote_copy(
-            src_ref=source,
-            dst_ref=target,
-            send_sem=self.send.at[index],
-            recv_sem=self.recv.at[index],
-            device_id={axis: peer},
-            device_id_type=pl.DeviceIdType.MESH,
-        )
-
-    def phases(self):
-        ref = self.ref
-        cx, cy = (ref.shape[0] - 2, ref.shape[1] - 2)
-        inner = ref.at[pl.ds(1, cx), pl.ds(1, cy)]
-        return (
-            (
-                self.copy(0, self.own, inner.at[:, :, 1], "gz", 1),
-                self.copy(1, self.own, inner.at[:, :, 2], "gz", -1),
-            ),
-            (
-                self.copy(2, ref.at[pl.ds(cx, 1), pl.ds(1, cy)], ref.at[pl.ds(0, 1), pl.ds(1, cy)], "gx", 1),
-                self.copy(3, ref.at[pl.ds(1, 1), pl.ds(1, cy)], ref.at[pl.ds(cx + 1, 1), pl.ds(1, cy)], "gx", -1),
-            ),
-            (
-                self.copy(4, ref.at[:, pl.ds(cy, 1)], ref.at[:, pl.ds(0, 1)], "gy", 1),
-                self.copy(5, ref.at[:, pl.ds(1, 1)], ref.at[:, pl.ds(cy + 1, 1)], "gy", -1),
-            ),
-        )
-
-
-def run_phase(copies, wait):
-    for copy in copies:
-        if wait:
-            copy.wait()
-        else:
-            copy.start()
+def edge(shift, cells):
+    if shift == 0:
+        return pl.ds(0, cells), pl.ds(1, cells)
+    if shift > 0:
+        return pl.ds(cells - 1, 1), pl.ds(0, 1)
+    return pl.ds(0, 1), pl.ds(cells + 1, 1)
 
 
 def exchange_kernel(sizes, own_ref, *refs):
     halo_ref, around_ref, sem, send_sem, recv_sem = refs[-5:]
     cells_x, cells_y, comps = own_ref.shape[:3]
     nx, ny = (cells_x + 2, cells_y + 2)
+    shifts = [
+        (x, y, z) for x in (0, 1, -1) for y in (0, 1, -1) for z in (0, 1, -1) if (x, y, z) != (0, 0, 0)
+    ]
+    peers = [
+        {axis: lax.rem(lax.axis_index(axis) + (step + sizes[axis]), sizes[axis]) for axis, step in zip(sizes, shift)}
+        for shift in shifts
+    ]
     barrier = pltpu.get_barrier_semaphore()
-    for axis, count in sizes.items():
-        for shift in (1, count - 1):
-            peer = lax.rem(lax.axis_index(axis) + shift, count)
-            pl.semaphore_signal(
-                barrier, inc=1, device_id={axis: peer}, device_id_type=pl.DeviceIdType.MESH
+    for peer in peers:
+        pl.semaphore_signal(barrier, inc=1, device_id=peer, device_id_type=pl.DeviceIdType.MESH)
+    keep = pltpu.make_async_copy(own_ref, around_ref.at[pl.ds(1, cells_x), pl.ds(1, cells_y), 0], sem)
+    keep.start()
+    pl.semaphore_wait(barrier, len(shifts))
+    copies = []
+    for index, (shift, peer) in enumerate(zip(shifts, peers)):
+        from_x, to_x = edge(shift[0], cells_x)
+        from_y, to_y = edge(shift[1], cells_y)
+        copies.append(
+            pltpu.make_async_remote_copy(
+                src_ref=own_ref.at[from_x, from_y],
+                dst_ref=around_ref.at[to_x, to_y, shift[2] % 3],
+                send_sem=send_sem.at[index],
+                recv_sem=recv_sem.at[index],
+                device_id=peer,
+                device_id_type=pl.DeviceIdType.MESH,
             )
-    keep = pltpu.make_async_copy(
-        own_ref, around_ref.at[pl.ds(1, cells_x), pl.ds(1, cells_y), 0], sem
-    )
-    keep.start()
-    pl.semaphore_wait(barrier, 2 * len(sizes))
-    phases = Exchange(sizes, own_ref, around_ref, send_sem, recv_sem).phases()
-    run_phase(phases[0], False)
+        )
+        copies[-1].start()
     keep.wait()
-    run_phase(phases[0], True)
-    for copies in phases[1:]:
-        run_phase(copies, False)
-        run_phase(copies, True)
+    for copy in copies:
+        copy.wait()
 
     lane_row = iota((1, LANES), 1)
     low_half = lane_row < SLOTS
@@ -290,8 +282,8 @@
         scratch_shapes=[
             pltpu.VMEM((nx, ny, 3, comps, LANES), jnp.float32),
             pltpu.SemaphoreType.DMA,
-            pltpu.SemaphoreType.DMA((6,)),
-            pltpu.SemaphoreType.DMA((6,)),
+            pltpu.SemaphoreType.DMA((26,)),
+            pltpu.SemaphoreType.DMA((26,)),
         ],
         compiler_params=pltpu.CompilerParams(
             vmem_limit_bytes=8 * 1024 * 1024, collective_id=number, has_side_effects=True

time: 74.7 us -> 72 us (0.964)
  Pallas kernels: 71.4 us -> 68 us
    pallas_call x2, Pallas kernels: 24.5 us -> 18.9 us  [call_exchange(): pl.pallas_call(functools.partial(exchange_kernel, sizes), out_shape=jax.S...]
    pallas_call x1, Pallas kernels: 24.7 us -> 26.4 us  [on_device(): pl.pallas_call(density_kernel, out_shape=(shape((cells_x, cells_y, 1, LAN...]
where the time goes in v3:
time: 72 us; the launch traced here: 70.6 us
  Pallas kernels  68 us (94%)
  local copies, waits for them, and re-layouts  1.14 us (2%)
  other arithmetic  0.77 us (1%)
    pallas_call x1, Pallas kernels, on_device(): pl.pallas_call(density_kernel, out_shape=(shape((cells_x, cells_y, 1, LAN...  26.4 us
    pallas_call x1, Pallas kernels, on_device(): pl.pallas_call(force_kernel, out_shape=(shape((3, columns, LANES), f32),...  22.7 us
    pallas_call x2, Pallas kernels, call_exchange(): pl.pallas_call(functools.partial(exchange_kernel, sizes), out_shape=jax.S...  18.9 us

profile of v3, /device:TPU:0, one launch (start us, length us, event | category | flops | bytes accessed | tf_op | source)
XLA Modules:
  0.0 70.6 jit_solution(16902789982092667072)
XLA Ops:
  0.6 0.1 iota.12
  0.7 0.8 %copy.7 = s32[4,4,2]{2,1,0:T(4,128)S(1)} copy(s32[4,4,2]{1,2,0:T(2,128)} %param.3) | data formatting | bytes 256 | tf_op args[1]
  1.5 0.1 reshape.23.own_ref
  1.6 0.1 lt.14
  1.7 0.1 lt.15
  1.8 0.8 %fusion.own_ref.placed_ref = f32[4,4,3,128]{3,2,1,0:T(4,128)S(1)} fusion(f32[3,4,4,128]{3,2,1,0:T(4,128)} %param.2, pred[4,4,128]{2,1,0:T(4,128)(4,1)S(1)} %broadcast_compare_fusion), kind=kLoop, calls=%fused_computation.1 | loop fusion | flops 6144 | bytes 51200 | tf_op jit(solution)/shard_map/transpose | solution.py:468
  2.6 10.0 %exchange.2.halo_ref = f32[36,8,128]{2,1,0:T(8,128)S(1)} custom-call(f32[4,4,3,128]{3,2,1,0:T(4,128)S(1)} %fusion.own_ref.placed_ref), custom_call_target="tpu_custom_call" | custom-call | tf_op jit(solution)/shard_map/exchange/pallas_call | solution.py:277
  12.6 26.4 %density.1 = (f32[4,4,1,128]{3,2,1,0:T(1,128)S(1)}, f32[16,128]{1,0:T(8,128)S(1)}, f32[576,8,128]{2,1,0:T(8,128)S(1)}, f32[640,8,128]{2,1,0:T(8,128)S(1)}, f32[1...) custom-call(s32[32]{0:T(128)S(1)} %reshape.23.own_ref, f32[4,4,3,128]{3,2,1,0:T(4,128)S(1)} %fusion.own_ref.placed_ref, ...), custom_call_target="tpu_custom_call" | custom-call | tf_op jit(solution)/shard_map/density/pallas_call | solution.py:489
  38.9 8.9 %exchange.3.halo_ref = f32[36,8,128]{2,1,0:T(8,128)S(1)} custom-call(f32[4,4,1,128]{3,2,1,0:T(1,128)S(1)} %get-tuple-element.10.own_ref.slope_own), custom_call_target="tpu_custom_call" | custom-call | tf_op jit(solution)/shard_map/exchange/pallas_call | solution.py:277
  47.9 22.7 %forces.1 = (f32[3,16,128]{2,1,0:T(8,128)}, f32[16,128]{1,0:T(8,128)}) custom-call(s32[32]{0:T(128)S(1)} %reshape.23.own_ref, f32[4,4,3,128]{3,2,1,0:T(4,128)S(1)} %fusion.own_ref.placed_ref, f32[4,4,1,128]{3,2,1,0:T(1,128)S(1)} %get-tuple-element.10.own_ref.slope_own, f32[16,128]{1,0:T(8,128)S(1)} %get-tuple-element.11.embed_ref, ...), custom_call_target="tpu_custom_call" | custom-call | tf_op jit(solution)/shard_map/forces/pallas_call | solution.py:499
  (2 shorter events, 0.0 us)

commit v4 on v3

--- a/solution.py
+++ b/solution.py
@@ -35,6 +35,7 @@
 LOG2E = math.log2(math.e)
 KEEP_SQUARED = 5.5075**2
 ROWS = 16
+DENSE_ROWS = 32
 WIDE = 2
 TILES = 20
 
@@ -97,38 +98,24 @@
                 gap = gap + pltpu.roll(gap, 2, 0)
                 data.append(value)
                 drops.append(gap >= KEEP_SQUARED)
-    dropped = [jnp.where(d, 1.0, 0.0) for d in drops]
-    groups = []
-    for first in range(0, 18, 4):
-        merged = dropped[first]
-        for k in range(first + 1, min(first + 4, 18)):
-            merged = jnp.where(comp == k - first, dropped[k], merged)
-        groups.append(merged)
-    sums = jnp.dot(
-        jnp.concatenate(groups, axis=0).astype(jnp.bfloat16), pre, preferred_element_type=jnp.float32
-    ).astype(jnp.int32)
-    moves = [
-        jnp.where(g > 0.5, 0, sums[8 * n : 8 * n + 8, :LANES]) for n, g in enumerate(groups)
-    ]
+    dropped = jnp.concatenate([jnp.where(d, 1.0, 0.0) for d in drops], axis=0).astype(jnp.bfloat16)
+    sums = jnp.dot(dropped, pre, preferred_element_type=jnp.float32).astype(jnp.int32)
+    moves = [jnp.where(drops[k], 0, sums[8 * k : 8 * k + 8, :LANES]) for k in range(18)]
     for bit in range(7):
         step = 1 << bit
-        for n in range(len(moves)):
-            move_in = pltpu.roll(moves[n], LANES - step, 1)
-            stay = jnp.where((moves[n] & step) != 0, 0, moves[n])
-            moves[n] = jnp.where((move_in & step) != 0, move_in, stay)
-    indices = [lane + move for move in moves]
-    for k in range(18):
-        index = jnp.where(comp == k % 4, indices[k // 4], 0)
-        index = index + pltpu.roll(index, 4, 0)
-        index = index + pltpu.roll(index, 2, 0)
-        data[k] = jnp.take_along_axis(data[k], index & (LANES - 1), axis=1, mode="promise_in_bounds")
+        for k in range(18):
+            value_in = pltpu.roll(data[k], LANES - step, 1)
+            move_in = pltpu.roll(moves[k], LANES - step, 1)
+            comes = (move_in & step) != 0
+            data[k] = jnp.where(comes, value_in, data[k])
+            moves[k] = jnp.where(comes, move_in, jnp.where((moves[k] & step) != 0, 0, moves[k]))
     counts = []
     one_row = iota((1, LANES), 1)
     for cz in (0, 1):
         line = jnp.zeros((1, LANES), jnp.int32)
         for k in range(9):
-            first = 2 * (9 * cz + k)
-            total = LANES - sums[first : first + 2, LANES:]
+            first = 8 * (9 * cz + k)
+            total = LANES - sums[first : first + 8, LANES:]
             line = jnp.where(one_row == 2 * k, total[0:1], line)
             line = jnp.where(one_row == 2 * k + 1, total[1:2], line)
         counts.append(line)
@@ -166,9 +153,7 @@
     scaled = jnp.minimum(radius * (1.0 / cut_width) - cut_radius / cut_width, 0.0)
     square = scaled * scaled
     quartic = square * square
-    bottom = 1.0 + quartic
-    inverse = pl.reciprocal(bottom, approx=True)
-    inverse = inverse * (2.0 - bottom * inverse)
+    inverse = pl.reciprocal(1.0 + quartic, approx=False)
     taper = quartic * inverse
     scale = math.sqrt(beta_one * LOG2E)
     along = radius * scale - radius_three * scale
@@ -219,8 +204,7 @@
     return pl.ds(0, 1), pl.ds(cells + 1, 1)
 
 
-def exchange_kernel(sizes, own_ref, *refs):
-    halo_ref, around_ref, sem, send_sem, recv_sem = refs[-5:]
+def exchange_kernel(sizes, own_ref, halo_ref, center_ref, around_ref, sem, send_sem, recv_sem):
     cells_x, cells_y, comps = own_ref.shape[:3]
     nx, ny = (cells_x + 2, cells_y + 2)
     shifts = [
@@ -251,6 +235,16 @@
             )
         )
         copies[-1].start()
+
+    @pl.loop(0, cells_x)
+    def _(x):
+        for y in range(cells_y):
+            value = own_ref[x, y]
+            for c in range(comps):
+                center_ref[x * cells_y + y, c] = jnp.transpose(
+                    jnp.broadcast_to(value[c : c + 1], (LANES, LANES))
+                )
+
     keep.wait()
     for copy in copies:
         copy.wait()
@@ -270,15 +264,18 @@
             halo_ref[x * ny + y] = jnp.concatenate(rows, axis=0)
 
 
-def call_exchange(sizes, own, number, held=()):
+def call_exchange(sizes, own, number):
     cells_x, cells_y, comps = own.shape[:3]
     nx, ny = (cells_x + 2, cells_y + 2)
     vmem = pl.BlockSpec(memory_space=pltpu.VMEM)
     return pl.pallas_call(
         functools.partial(exchange_kernel, sizes),
-        out_shape=jax.ShapeDtypeStruct((nx * ny, 8, LANES), jnp.float32),
-        in_specs=[vmem] + [pl.BlockSpec(memory_space=pl.ANY)] * len(held),
-        out_specs=vmem,
+        out_shape=(
+            jax.ShapeDtypeStruct((nx * ny, 8, LANES), jnp.float32),
+            jax.ShapeDtypeStruct((cells_x * cells_y, comps, LANES, LANES), jnp.float32),
+        ),
+        in_specs=[vmem],
+        out_specs=(vmem, vmem),
         scratch_shapes=[
             pltpu.VMEM((nx, ny, 3, comps, LANES), jnp.float32),
             pltpu.SemaphoreType.DMA,
@@ -289,18 +286,18 @@
             vmem_limit_bytes=8 * 1024 * 1024, collective_id=number, has_side_effects=True
         ),
         name="exchange",
-    )(own, *held)
+    )(own)
 
 
 def density_kernel(
     own_ref,
     placed_ref,
     halo_ref,
+    center_ref,
     slope_ref,
     embed_ref,
     packed_ref,
     list_ref,
-    center_ref,
     count_vmem,
     count_ref,
     length_ref,
@@ -313,12 +310,6 @@
 
     @pl.loop(0, columns)
     def _(column):
-        value = placed_ref[column // cells_y, column % cells_y]
-        for c in range(3):
-            center_ref[column, c] = jnp.transpose(jnp.broadcast_to(value[c : c + 1], (LANES, LANES)))
-
-    @pl.loop(0, columns)
-    def _(column):
         outs, counts = compress_cells(halo_ref, column // cells_y, column % cells_y, ny)
         for k in range(18):
             packed_ref[column * 36 + 2 * k] = outs[k]
@@ -341,13 +332,13 @@
         column = cell // 2
         begin = (cell % 2) * SLOTS
         steps = length_ref[cell]
-        blocks = (own_ref[cell] + ROWS - 1) // ROWS
+        blocks = (own_ref[cell] + DENSE_ROWS - 1) // DENSE_ROWS
 
         @pl.loop(0, blocks)
         def _(block):
-            start = pl.multiple_of(begin + block * ROWS, ROWS)
+            start = pl.multiple_of(begin + block * DENSE_ROWS, DENSE_ROWS)
             centers = [
-                jnp.concatenate([center_ref[column, c, pl.ds(start, ROWS), :]] * WIDE, axis=1) for c in range(3)
+                jnp.concatenate([center_ref[column, c, pl.ds(start, DENSE_ROWS), :]] * WIDE, axis=1) for c in range(3)
             ]
 
             def step(index, sums):
@@ -356,9 +347,9 @@
                 )
                 return (sums[0] + fold(pair_parts(centers, tile)[0]),)
 
-            zero = jnp.zeros((ROWS, LANES), jnp.float32)
+            zero = jnp.zeros((DENSE_ROWS, LANES), jnp.float32)
             sums = lax.fori_loop(0, steps, step, (zero,))
-            sum_ref[0, column, pl.ds(start, ROWS), :] = sums[0]
+            sum_ref[0, column, pl.ds(start, DENSE_ROWS), :] = sums[0]
 
     filled = jnp.concatenate(
         [placed_ref[c // cells_y, c % cells_y, 0:1] for c in range(columns)], axis=0
@@ -374,18 +365,17 @@
 def force_kernel(
     own_ref,
     placed_ref,
-    slope_own,
     embed_ref,
     halo_ref,
+    slope_center,
+    center_ref,
     packed_in,
     list_ref,
-    center_ref,
     count_vmem,
     force_ref,
     energy_ref,
     packed_ref,
     slope_list,
-    slope_center,
     count_ref,
     length_ref,
     sum_ref,
@@ -402,11 +392,6 @@
 
     @pl.loop(0, columns)
     def _(column):
-        value = slope_own[column // cells_y, column % cells_y]
-        slope_center[column] = jnp.transpose(jnp.broadcast_to(value, (LANES, LANES)))
-
-    @pl.loop(0, columns)
-    def _(column):
         cx, cy = (column // cells_y, column % cells_y)
         for k in range(9):
             value = halo_ref[(cx + k // 3) * ny + cy + k % 3]
@@ -438,7 +423,7 @@
             centers = [
                 jnp.concatenate([center_ref[column, c, pl.ds(start, ROWS), :]] * WIDE, axis=1) for c in range(3)
             ]
-            slope_i = jnp.concatenate([slope_center[column, pl.ds(start, ROWS), :]] * WIDE, axis=1)
+            slope_i = jnp.concatenate([slope_center[column, 0, pl.ds(start, ROWS), :]] * WIDE, axis=1)
 
             def step(index, sums):
                 at = [cell * TILES + index * WIDE + k for k in range(WIDE)]
@@ -473,7 +458,7 @@
     f32 = jnp.float32
     shape = jax.ShapeDtypeStruct
     params = pltpu.CompilerParams(vmem_limit_bytes=24 * 1024 * 1024)
-    halo = call_exchange(sizes, placed, 0)
+    halo, center = call_exchange(sizes, placed, 0)
     work = [
         pltpu.SMEM((cells, LANES), jnp.int32),
         pltpu.SMEM((cells,), jnp.int32),
@@ -483,19 +468,18 @@
     saved = (
         shape((cells * 18, 8, LANES), f32),
         shape((cells * TILES, 8, LANES), f32),
-        shape((columns, 3, LANES, LANES), f32),
         shape((cells, LANES), jnp.int32),
     )
     slope, embed, *kept = pl.pallas_call(
         density_kernel,
         out_shape=(shape((cells_x, cells_y, 1, LANES), f32), shape((columns, LANES), f32)) + saved,
-        in_specs=[smem, vmem, vmem],
-        out_specs=(vmem,) * 6,
+        in_specs=[smem, vmem, vmem, vmem],
+        out_specs=(vmem,) * 5,
         scratch_shapes=work,
         compiler_params=params,
         name="density",
-    )(own, placed, halo)
-    halo = call_exchange(sizes, slope, 1)
+    )(own, placed, halo, center)
+    halo, slope_center = call_exchange(sizes, slope, 1)
     forces, energy = pl.pallas_call(
         force_kernel,
         out_shape=(shape((3, columns, LANES), f32), shape((columns, LANES), f32)),
@@ -504,12 +488,11 @@
         scratch_shapes=[
             pltpu.VMEM((cells * 18, 8, LANES), f32),
             pltpu.VMEM((cells * TILES, 8, LANES), f32),
-            pltpu.VMEM((columns, LANES, LANES), f32),
         ]
         + work,
         compiler_params=params,
         name="forces",
-    )(own, placed, slope, embed, halo, *kept)
+    )(own, placed, embed, halo, slope_center, center, *kept)
     return (
         forces.reshape(3, cells_x, cells_y, cells_z * SLOTS),
         energy.reshape(cells_x, cells_y, cells_z * SLOTS),

time: 72 us -> 63.2 us (0.88)
  Pallas kernels: 68 us -> 59.6 us
    pallas_call x1, Pallas kernels: 26.4 us -> 20.9 us  [on_device(): pl.pallas_call(density_kernel, out_shape=(shape((cells_x, cells_y, 1, LAN...]
    pallas_call x1, Pallas kernels: 22.7 us -> 20.6 us  [on_device(): pl.pallas_call(force_kernel, out_shape=(shape((3, columns, LANES), f32),...]
    pallas_call x2, Pallas kernels: 18.9 us -> 18.1 us  [call_exchange(): pl.pallas_call(functools.partial(exchange_kernel, sizes), out_shape=(jax....]
where the time goes in v4:
time: 63.2 us; the launch traced here: 62.1 us
  Pallas kernels  59.6 us (94%)
  local copies, waits for them, and re-layouts  1.14 us (2%)
  other arithmetic  0.77 us (1%)
  between operations  0.67 us (1%)
    pallas_call x1, Pallas kernels, on_device(): pl.pallas_call(density_kernel, out_shape=(shape((cells_x, cells_y, 1, LAN...  20.9 us
    pallas_call x1, Pallas kernels, on_device(): pl.pallas_call(force_kernel, out_shape=(shape((3, columns, LANES), f32),...  20.6 us
    pallas_call x2, Pallas kernels, call_exchange(): pl.pallas_call(functools.partial(exchange_kernel, sizes), out_shape=(jax....  18.1 us

profile of v4, /device:TPU:0, one launch (start us, length us, event | category | flops | bytes accessed | tf_op | source)
XLA Modules:
  0.0 62.1 jit_solution(16000261652873629896)
XLA Ops:
  0.6 0.1 iota.12
  0.7 0.8 %copy.7 = s32[4,4,2]{2,1,0:T(4,128)S(1)} copy(s32[4,4,2]{1,2,0:T(2,128)} %param.3) | data formatting | bytes 256 | tf_op args[1]
  1.5 0.1 reshape.23.own_ref
  1.6 0.1 lt.14
  1.7 0.1 lt.15
  1.8 0.8 %fusion.own_ref.placed_ref = f32[4,4,3,128]{3,2,1,0:T(4,128)S(1)} fusion(f32[3,4,4,128]{3,2,1,0:T(4,128)} %param.2, pred[4,4,128]{2,1,0:T(4,128)(4,1)S(1)} %broadcast_compare_fusion), kind=kLoop, calls=%fused_computation.1 | loop fusion | flops 6144 | bytes 51200 | tf_op jit(solution)/shard_map/transpose | solution.py:453
  2.6 10.0 %exchange.2 = (f32[36,8,128]{2,1,0:T(8,128)S(1)}, f32[16,3,128,128]{3,2,1,0:T(8,128)S(1)}) custom-call(f32[4,4,3,128]{3,2,1,0:T(4,128)S(1)} %fusion.own_ref.placed_ref), custom_call_target="tpu_custom_call" | custom-call | tf_op jit(solution)/shard_map/exchange/pallas_call | solution.py:271
  12.6 20.9 %density.1 = (f32[4,4,1,128]{3,2,1,0:T(1,128)S(1)}, f32[16,128]{1,0:T(8,128)S(1)}, f32[576,8,128]{2,1,0:T(8,128)S(1)}, f32[640,8,128]{2,1,0:T(8,128)S(1)}, s32[32,128]{1,0:T(8,128)S(1)}) custom-call(s32[32]{0:T(128)S(1)} %reshape.23.own_ref, f32[4,4,3,128]{3,2,1,0:T(4,128)S(1)} %fusion.own_ref.placed_ref, f32[36,8,128]{2,1,0:T(8,128)S(1)} %get-tuple-element.13.halo_ref, ...), custom_call_target="tpu_custom_call" | custom-call | tf_op jit(solution)/shard_map/density/pallas_call | solution.py:473
  33.4 8.1 %exchange.3 = (f32[36,8,128]{2,1,0:T(8,128)S(1)}, f32[16,1,128,128]{3,2,1,0:T(8,128)S(1)}) custom-call(f32[4,4,1,128]{3,2,1,0:T(1,128)S(1)} %get-tuple-element.16.own_ref), custom_call_target="tpu_custom_call" | custom-call | tf_op jit(solution)/shard_map/exchange/pallas_call | solution.py:271
  41.6 20.6 %forces.1 = (f32[3,16,128]{2,1,0:T(8,128)}, f32[16,128]{1,0:T(8,128)}) custom-call(s32[32]{0:T(128)S(1)} %reshape.23.own_ref, f32[4,4,3,128]{3,2,1,0:T(4,128)S(1)} %fusion.own_ref.placed_ref, f32[16,128]{1,0:T(8,128)S(1)} %get-tuple-element.15.embed_ref, f32[36,8,128]{2,1,0:T(8,128)S(1)} %get-tuple-element.17.halo_ref, ...), custom_call_target="tpu_custom_call" | custom-call | tf_op jit(solution)/shard_map/forces/pallas_call | solution.py:483
  (2 shorter events, 0.0 us)
